TPU v7x, 32 devices: a whole 2x2x4 slice. The times are simulated.
32 devices in a mesh: tm: 4 (over y, x), paths: 8 (over z, core).
Axes of the slice: x: 2, y: 2, z: 4, core: 2. Of those that a mesh axis runs over, the one named last changes fastest.
Arguments:
- returns: bfloat16 [128, 4096, 256], P('tm', 'paths'), may hold values from -0.15917969 to 0.15917969
- weights: bfloat16 [256, 64], P('paths'), may hold values from -0.375 to 0.375
Outputs:
- drawdown: float32 [64, 4096], P('tm', 'paths')
All inputs are finite; a program needn't handle non-finite values.
Results may differ from a plain program's by a relative error of at most 0.0003.
Values may be sent and summed in bfloat16 or wider, within the bound.
No kernel may reach another device: no remote copies, remote signals or barrier semaphores. Data moves between devices by JAX's collectives and lax.ppermute only.
A program may use at most 64 MiB of HBM per device.

v0:
```python
import jax
import jax.numpy as jnp
from jax import lax
from jax.sharding import PartitionSpec as P

very_large = 1e30


def prefix(part, axis, combine, identity):
    place = lax.axis_index(axis)
    gathered = jax.tree.map(lambda a: lax.all_gather(a, axis), part)
    state = jax.tree.map(lambda a, e: jnp.zeros_like(a) + jnp.asarray(e, a.dtype), part, identity)

    def one(lap, state):
        return combine(
            state, jax.tree.map(lambda a: lax.dynamic_index_in_dim(a, lap, 0, False), gathered)
        )

    return lax.fori_loop(0, place, one, state)


def join_two(earlier, later):
    return (earlier[0] + later[0], jnp.maximum(earlier[1], earlier[0] + later[1]))


def shards(returns, weights):
    all_weights = lax.all_gather(weights, "paths", axis=0, tiled=True)
    profit = jnp.einsum("tpa,aq->tqp", returns, all_weights, preferred_element_type=jnp.float32)
    steps_here = profit.shape[0]
    row_ids = lax.broadcasted_iota(jnp.int32, (steps_here, steps_here), 0)
    col_ids = lax.broadcasted_iota(jnp.int32, (steps_here, steps_here), 1)
    lower = (row_ids >= col_ids).astype(jnp.float32)
    flat = profit.reshape(steps_here, -1)
    values = jnp.dot(
        lower, flat, precision=lax.Precision.HIGHEST, preferred_element_type=jnp.float32
    ).reshape(profit.shape)
    peaks = jnp.maximum(lax.cummax(values, axis=0), 0.0)
    offset = values[-1]
    highest = peaks[-1]
    segments = lax.axis_size("tm")
    block_width = offset.shape[0] // segments
    zeros = jnp.zeros_like(offset)
    prior_offset, prior_peak = prefix(
        (offset, highest), "tm", join_two, (zeros, zeros - very_large)
    )
    running = jnp.maximum(prior_peak[None], prior_offset[None] + peaks)
    falls = jnp.max(running - (prior_offset[None] + values), axis=0)
    blocks = falls.reshape(segments, block_width, falls.shape[1])
    received = lax.all_to_all(blocks, "tm", split_axis=0, concat_axis=0, tiled=True)
    return jnp.max(received, axis=0)


def solution(mesh):
    in_specs = (P("tm", "paths", None), P("paths", None))
    out_specs = P("tm", "paths")
    return jax.shard_map(shards, mesh=mesh, in_specs=in_specs, out_specs=out_specs, check_vma=False)
```

profile of v0, /device:TPU:0, one launch (start us, length us, event | category | flops | bytes accessed | tf_op | source)
XLA Modules:
  0.0 87.8 jit_solution(8947005105098982368)
XLA Ops:
  0.0 15.9 %all_gather.9 = bf16[256,64]{1,0:T(8,128)(2,1)S(1)} all-gather(bf16[32,64]{1,0:T(8,128)(2,1)} %param.5), channel_id=1, replica_groups=mesh['tm'=4,'paths'=8] {'paths'}, dimensions={0}, use_global_device_ids=true | all-gather | bytes 36864 | tf_op jit(solution)/shard_map/all_gather | solution.py:27
  15.9 6.0 %fusion.1 = f32[64,32,512]{2,0,1:T(8,128)S(1)} fusion(bf16[32,512,256]{2,1,0:T(8,128)(2,1)} %param.4, bf16[256,64]{1,0:T(8,128)(2,1)S(1)} %all_gather.9), kind=kOutput, calls=%fused_computation.6 | convolution fusion | flops 536870912 | bytes 12615680 | tf_op jit(solution)/shard_map/tpa,aq->tqp/dot_general | solution.py:28
  21.9 2.4 %copy.3 = f32[4,8,64,512]{3,1,2,0:T(8,128)S(1)} copy(f32[4,8,64,512]{3,2,1,0:T(8,128)S(1)} %bitcast.27) | data formatting | bytes 8388608
  24.4 2.1 %fusion.3 = f32[32,32768]{1,0:T(8,128)S(1)} fusion(f32[32,32768]{1,0:T(8,128)S(1)} %bitcast.29), kind=kOutput, calls=%fused_computation.9 | convolution fusion | flops 402654208 | bytes 8388608 | tf_op jit(solution)/shard_map/dot_general | solution.py:34
  26.5 0.0 copy-start
  26.5 0.4 slice_reduce_fusion
  26.9 2.4 %copy.4 = f32[4,8,64,512]{3,2,1,0:T(8,128)S(1)} copy(f32[4,8,64,512]{3,1,2,0:T(8,128)S(1)} %bitcast.25) | data formatting | bytes 8388608
  29.3 0.0 copy-done
  29.3 20.9 %broadcast_maximum_fusion = f32[32,64,512]{2,1,0:T(8,128)S(1)} fusion(f32[32,64,512]{2,1,0:T(8,128)S(1)} %bitcast.30), kind=kOutput, calls=%fused_computation.4 | output fusion | flops 33554432 | bytes 8388608 | tf_op jit(solution)/shard_map/shards/reduce_window_max | solution.py:37
  50.2 0.0 copy-start.2
  50.2 2.0 %copy-done.2 = f32[32,64,512]{2,1,0:T(8,128)} copy-done((f32[32,64,512]{2,1,0:T(8,128)}, f32[32,64,512]{2,1,0:T(8,128)S(1)}, u32[]{:S(2)}) %copy-start.2) | copy-done | bytes 4194328
  52.2 10.3 %all_gather.11 = f32[4,64,512]{2,1,0:T(8,128)S(1)} all-gather(f32[1,64,512]{2,1,0:T(8,128)S(1)} %slice.13), channel_id=1, replica_groups=mesh['tm'=4,'paths'=8] {'tm'}, dimensions={0}, use_global_device_ids=true | all-gather | bytes 655360 | tf_op jit(solution)/shard_map/all_gather | solution.py:11
  62.6 10.7 %all_gather.10 = f32[4,64,512]{2,1,0:T(8,128)S(1)} all-gather(f32[1,64,512]{2,1,0:T(8,128)S(1)} %slice.10), channel_id=1, replica_groups=mesh['tm'=4,'paths'=8] {'tm'}, dimensions={0}, use_global_device_ids=true | all-gather | bytes 655360 | tf_op jit(solution)/shard_map/all_gather | solution.py:11
  73.3 0.2 while.12
  73.6 0.0 copy-start.1
  73.6 4.8 %copy.7 = f32[4,8,64,512]{3,1,2,0:T(8,128)S(1)} copy(f32[4,8,64,512]{3,2,1,0:T(8,128)} %bitcast.26) | data formatting | bytes 8388608
  78.4 0.0 copy-done.1
  78.4 0.9 %subtract_reduce_fusion = f32[32768]{0:T(1024)S(1)} fusion(f32[32,32768]{1,0:T(8,128)S(1)} %copy-done.1, f32[32,32768]{1,0:T(8,128)S(1)} %bitcast.28, f32[32768]{0:T(1024)S(1)} %bitcast.33, f32[32768]{0:T(1024)S(1)} %bitcast.34), kind=kLoop, calls=%fused_computation.3 | loop fusion | flops 5210112 | bytes 8781824 | tf_op jit(solution)/shard_map/reduce_max | solution.py:47
  79.4 7.8 %all_to_all.5 = f32[4,16,512]{2,1,0:T(8,128)S(1)} all-to-all(f32[4,16,512]{2,1,0:T(8,128)S(1)} %reshape.24), channel_id=1, replica_groups=mesh['tm'=4,'paths'=8] {'tm'}, dimensions={0} | all-to-all | bytes 262144 | tf_op jit(solution)/shard_map/all_to_all | solution.py:49
  87.2 0.6 reduce_max.19
  (7 shorter events, 0.1 us)
Async XLA Ops:
  26.5 2.8 %copy-start = (f32[32,32768]{1,0:T(8,128)}, f32[32,32768]{1,0:T(8,128)S(1)}, u32[]{:S(2)}) copy-start(f32[32,32768]{1,0:T(8,128)S(1)} %fusion.3) | copy-start | bytes 12582916
  50.2 2.0 %copy-start.2 = (f32[32,64,512]{2,1,0:T(8,128)}, f32[32,64,512]{2,1,0:T(8,128)S(1)}, u32[]{:S(2)}) copy-start(f32[32,64,512]{2,1,0:T(8,128)S(1)} %broadcast_maximum_fusion) | copy-start | bytes 12582916
  73.6 4.8 %copy-start.1 = (f32[32,32768]{1,0:T(8,128)S(1)}, f32[32,32768]{1,0:T(8,128)}, u32[]{:S(2)}) copy-start(f32[32,32768]{1,0:T(8,128)} %copy-done) | copy-start | bytes 12582916
where the time goes:
time: 88.1 us; the launch traced here: 87.8 us
  blocking collectives  44.8 us (51%)
  other arithmetic  22.5 us (26%)
  local copies, waits for them, and re-layouts  12.1 us (14%)
  matrix products  8.14 us (9%)
    all_gather x2, blocking collectives, prefix(): gathered = jax.tree.map(lambda a: lax.all_gather(a, axis), part)  21 us
    another operation x1, other arithmetic, shards(): peaks = jnp.maximum(lax.cummax(values, axis=0), 0.0)  20.9 us
    all_gather x1, blocking collectives, shards(): all_weights = lax.all_gather(weights, 'paths', axis=0, tiled=True)  15.9 us
    unnamed x11, local copies, waits for them, and re-layouts  11.7 us
    all_to_all x1, blocking collectives, shards(): lax.all_to_all(blocks, 'tm', split_axis=0, concat_axis=0, tiled=True)  7.85 us
    dot_general x1, matrix products, shards(): jnp.einsum('tpa,aq->tqp', returns, all_weights, preferred_element_type=jn...  6.03 us
    dot_general x1, matrix products, shards(): jnp.dot(lower, flat, precision=lax.Precision.HIGHEST, preferred_element_t...  2.11 us

commit v1 on v0

v1 whole, which is shorter than its diff:
```python
import functools

import jax
import jax.numpy as jnp
from jax import lax
from jax.experimental import pallas as pl
from jax.experimental.pallas import tpu as pltpu
from jax.sharding import PartitionSpec as P


def gather_weights(weights):
    count = lax.axis_size("paths")
    place = lax.axis_index("paths")
    rows = weights
    step = 1
    while step < count:
        other = lax.ppermute(rows, "paths", [(s, s ^ step) for s in range(count)])
        low = (place & step) == 0
        rows = jnp.where(low, jnp.concatenate([rows, other]), jnp.concatenate([other, rows]))
        step *= 2
    return rows


def segment_kernel(segments, tile, weights_ref, returns_ref, *refs):
    outs = refs[:segments]
    block, arrived, stats = refs[segments:]
    steps, paths, assets = returns_ref.shape
    ports = weights_ref.shape[1]
    width = ports // segments

    def fetch(t):
        return pltpu.make_async_copy(returns_ref.at[t], block.at[t], arrived.at[t])

    for t in range(steps):
        fetch(t).start()

    own = lax.axis_index("tm")
    row = lax.broadcasted_iota(jnp.int32, (ports, ports), 0)
    col = lax.broadcasted_iota(jnp.int32, (ports, ports), 1)
    pick = col == ((row // width) ^ own) * width + row % width
    contract_last = (((1,), (1,)), ((), ()))
    turned = lax.dot_general(
        pick.astype(jnp.bfloat16), weights_ref[...], contract_last,
        preferred_element_type=jnp.float32,
    ).astype(jnp.bfloat16)

    stats[...] = jnp.zeros_like(stats)
    lanes = min(256, paths)

    def group(g, carry):
        first = g * tile
        for i in range(tile):
            fetch(first + i).wait()
        for c in range(0, paths, lanes):
            profits = [
                lax.dot_general(
                    turned, block[first + i, c : c + lanes, :], contract_last,
                    preferred_element_type=jnp.float32,
                )
                for i in range(tile)
            ]
            for q in range(0, ports, 16):
                at = (pl.ds(q, 16), pl.ds(c, lanes))
                value, peak, low, fall = (stats[(n, *at)] for n in range(4))
                for i in range(tile):
                    value = value + profits[i][q : q + 16]
                    peak = jnp.maximum(peak, value)
                    low = jnp.minimum(low, value)
                    fall = jnp.maximum(fall, peak - value)
                for n, new in enumerate((value, peak, low, fall)):
                    stats[(n, *at)] = new
        return carry

    lax.fori_loop(0, steps // tile, group, 0)

    for k in range(segments):
        at = slice(k * width, (k + 1) * width)
        outs[k][0] = stats[3, at]
        outs[k][1] = stats[2, at]
        outs[k][2] = stats[1, at] - stats[0, at]
        outs[k][3] = stats[0, at]


def join_kernel(segments, *refs):
    ins, out_ref, ordered = refs[:segments], refs[segments], refs[segments + 1]
    own = lax.axis_index("tm")
    for k in range(segments):
        ordered[own ^ k] = ins[k][...]
    fall = ordered[0, 0]
    drop = ordered[0, 2]
    for s in range(1, segments):
        fall = jnp.maximum(jnp.maximum(fall, ordered[s, 0]), drop - ordered[s, 1])
        drop = jnp.maximum(drop - ordered[s, 3], ordered[s, 2])
    out_ref[...] = fall


def shards(returns, weights):
    segments = lax.axis_size("tm")
    steps, paths, assets = returns.shape
    ports = weights.shape[1]
    width = ports // segments
    tile = 8 if steps % 8 == 0 else 1
    part = jax.ShapeDtypeStruct((4, width, paths), jnp.float32)
    vmem = pl.BlockSpec(memory_space=pltpu.VMEM)
    all_weights = gather_weights(weights)
    parts = pl.pallas_call(
        functools.partial(segment_kernel, segments, tile),
        out_shape=[part] * segments,
        in_specs=[vmem, pl.BlockSpec(memory_space=pltpu.HBM)],
        out_specs=[vmem] * segments,
        scratch_shapes=[
            pltpu.VMEM((steps, paths, assets), returns.dtype),
            pltpu.SemaphoreType.DMA((steps,)),
            pltpu.VMEM((4, ports, paths), jnp.float32),
        ],
        compiler_params=pltpu.CompilerParams(vmem_limit_bytes=24 * 2**20),
        name="segment",
    )(all_weights, returns)
    arrived = [parts[0]] + [
        lax.ppermute(parts[k], "tm", [(s, s ^ k) for s in range(segments)])
        for k in range(1, segments)
    ]
    return pl.pallas_call(
        functools.partial(join_kernel, segments),
        out_shape=jax.ShapeDtypeStruct((width, paths), jnp.float32),
        in_specs=[vmem] * segments,
        out_specs=vmem,
        scratch_shapes=[pltpu.VMEM((segments, 4, width, paths), jnp.float32)],
        compiler_params=pltpu.CompilerParams(vmem_limit_bytes=8 * 2**20),
        name="join",
    )(*arrived)


def solution(mesh):
    in_specs = (P("tm", "paths", None), P("paths", None))
    out_specs = P("tm", "paths")
    return jax.shard_map(shards, mesh=mesh, in_specs=in_specs, out_specs=out_specs, check_vma=False)
```

time: 88.1 us -> 29.9 us (0.34)
  blocking collectives: 44.8 us -> 0 us
  other arithmetic: 22.5 us -> 0.81 us
  waiting for transfers between devices: 0 us -> 10.4 us
  starting transfers between devices: 0 us -> 10.1 us
  local copies, waits for them, and re-layouts: 12.1 us -> 3.38 us
  matrix products: 8.14 us -> 0 us
  Pallas kernels: 0 us -> 4.87 us
    all_gather x3 -> x0, blocking collectives: 36.9 us -> none  [the longest x2 21 us: prefix(): gathered = jax.tree.map(lambda a: lax.all_gather(a, axis), part)]
    another operation x1 -> x0, other arithmetic: 20.9 us -> none  [shards(): peaks = jnp.maximum(lax.cummax(values, axis=0), 0.0)]
    ppermute x0 -> x6, waiting for transfers between devices: none -> 10.4 us  [the longest x3 5.72 us: shards(): lax.ppermute(parts[k], 'tm', [(s, s ^ k) for s in range(segments)])]
    ppermute x0 -> x6, starting transfers between devices: none -> 10.1 us  [the longest x3 6.55 us: gather_weights(): other = lax.ppermute(rows, 'paths', [(s, s ^ step) for s in range(count)])]
    unnamed x11 -> x2, local copies, waits for them, and re-layouts: 11.7 us -> 3.38 us
    dot_general x2 -> x0, matrix products: 8.14 us -> none  [the longest x1 6.03 us: shards(): jnp.einsum('tpa,aq->tqp', returns, all_weights, preferred_element_type=jn...]
    all_to_all x1 -> x0, blocking collectives: 7.85 us -> none  [shards(): lax.all_to_all(blocks, 'tm', split_axis=0, concat_axis=0, tiled=True)]
    pallas_call x0 -> x2, Pallas kernels: none -> 4.87 us  [the longest x1 4.19 us: shards(): pl.pallas_call(functools.partial(segment_kernel, segments, tile), out_sha...]
  transfers between devices with their start and end apart: 0 -> 6, of which waited for: 0 -> 6; matrix products, arithmetic and copies ran while one was open for 0% -> 0% of each run, Pallas kernels for 0% -> 0%
where the time goes in v1:
time: 29.9 us; the launch traced here: 29.6 us
  waiting for transfers between devices  10.4 us (35%)
  starting transfers between devices  10.1 us (34%)
  Pallas kernels  4.87 us (16%)
  local copies, waits for them, and re-layouts  3.38 us (11%)
  other arithmetic  0.81 us (3%)
    ppermute x3, starting transfers between devices, gather_weights(): other = lax.ppermute(rows, 'paths', [(s, s ^ step) for s in range(count)])  6.55 us
    ppermute x3, waiting for transfers between devices, shards(): lax.ppermute(parts[k], 'tm', [(s, s ^ k) for s in range(segments)])  5.72 us
    ppermute x3, waiting for transfers between devices, gather_weights(): other = lax.ppermute(rows, 'paths', [(s, s ^ step) for s in range(count)])  4.65 us
    pallas_call x1, Pallas kernels, shards(): pl.pallas_call(functools.partial(segment_kernel, segments, tile), out_sha...  4.19 us
    ppermute x3, starting transfers between devices, shards(): lax.ppermute(parts[k], 'tm', [(s, s ^ k) for s in range(segments)])  3.55 us
    unnamed x2, local copies, waits for them, and re-layouts  3.38 us
    select_n x3, other arithmetic, gather_weights(): jnp.where(low, jnp.concatenate([rows, other]), jnp.concatenate([other, ro...  0.81 us
    pallas_call x1, Pallas kernels, shards(): pl.pallas_call(functools.partial(join_kernel, segments), out_shape=jax.Sh...  0.68 us
  transfers between devices with their start and end apart: 6, of which 6 were waited for; matrix products, arithmetic and copies ran while one was open for 0% of the time, Pallas kernels for 0%

profile of v1, /device:TPU:0, one launch (start us, length us, event | category | flops | bytes accessed | tf_op | source)
XLA Modules:
  0.0 29.6 jit_solution(14815861482512580087)
XLA Ops:
  0.0 0.5 %collective-permute-start = (bf16[32,64]{1,0:T(8,128)(2,1)}, bf16[32,64]{1,0:T(8,128)(2,1)S(1)}, u32[]{:S(2)}, u32[]{:S(2)}) collective-permute-start(bf16[32,64]{1,0:T(8,128)(2,1)} %param.3), channel_id=1, source_target_pairs={{0,1},{1,0},{2,3},{3,2},{4,5},{5,4},{6,7},{7,6},{8,9},{9,8},{10,11... | collective-permute-start | bytes 12296 | tf_op jit(solution)/shard_map/ppermute | solution.py:17
  0.5 1.0 %collective-permute-done = bf16[32,64]{1,0:T(8,128)(2,1)S(1)} collective-permute-done((bf16[32,64]{1,0:T(8,128)(2,1)}, bf16[32,64]{1,0:T(8,128)(2,1)S(1)}, u32[]{:S(2)}, u32[]{:S(2)}) %collective-permute-start) | collective-permute-done | bytes 4128 | tf_op jit(solution)/shard_map/ppermute | solution.py:17
  1.5 0.8 %maximum_select_fusion.2 = bf16[64,64]{1,0:T(8,128)(2,1)S(1)} fusion(bf16[32,64]{1,0:T(8,128)(2,1)S(1)} %collective-permute-done, bf16[32,64]{1,0:T(8,128)(2,1)} %param.3, pred[]{:T(512)S(6)} %eq.11), kind=kLoop, calls=%fused_computation.2 | loop fusion | flops 36864 | bytes 16385 | tf_op jit(solution)/shard_map/jit(_where)/select_n | solution.py:19
  2.3 3.0 %collective-permute-start.1 = (bf16[64,64]{1,0:T(8,128)(2,1)S(1)}, bf16[64,64]{1,0:T(8,128)(2,1)S(1)}, u32[]{:S(2)}, u32[]{:S(2)}) collective-permute-start(bf16[64,64]{1,0:T(8,128)(2,1)S(1)} %maximum_select_fusion.2), channel_id=1, source_target_pairs={{0,2},{1,3},{2,0},{3,1},{4,6},{5,7},{6,4},{7,5},{8,10},{9,11},{10,... | collective-permute-start | bytes 24584 | tf_op jit(solution)/shard_map/ppermute | solution.py:17
  5.3 1.7 %collective-permute-done.1 = bf16[64,64]{1,0:T(8,128)(2,1)S(1)} collective-permute-done((bf16[64,64]{1,0:T(8,128)(2,1)S(1)}, bf16[64,64]{1,0:T(8,128)(2,1)S(1)}, u32[]{:S(2)}, u32[]{:S(2)}) %collective-permute-start.1) | collective-permute-done | bytes 8224 | tf_op jit(solution)/shard_map/ppermute | solution.py:17
  7.0 3.1 %collective-permute-start.2 = (bf16[128,64]{1,0:T(8,128)(2,1)S(1)}, bf16[128,64]{1,0:T(8,128)(2,1)S(1)}, u32[]{:S(2)}, u32[]{:S(2)}) collective-permute-start(bf16[128,64]{1,0:T(8,128)(2,1)S(1)} %maximum_select_fusion.1), channel_id=1, source_target_pairs={{0,4},{1,5},{2,6},{3,7},{4,0},{5,1},{6,2},{7,3},{8,12},{9,13},{10,... | collective-permute-start | bytes 49160 | tf_op jit(solution)/shard_map/ppermute | solution.py:17
  10.1 1.9 %collective-permute-done.2 = bf16[128,64]{1,0:T(8,128)(2,1)S(1)} collective-permute-done((bf16[128,64]{1,0:T(8,128)(2,1)S(1)}, bf16[128,64]{1,0:T(8,128)(2,1)S(1)}, u32[]{:S(2)}, u32[]{:S(2)}) %collective-permute-start.2) | collective-permute-done | bytes 16416 | tf_op jit(solution)/shard_map/ppermute | solution.py:17
  12.0 0.0 copy-start
  12.0 3.4 %copy-done = bf16[32,512,256]{2,1,0:T(8,128)(2,1)S(1)} copy-done((bf16[32,512,256]{2,1,0:T(8,128)(2,1)S(1)}, bf16[32,512,256]{2,1,0:T(8,128)(2,1)}, u32[]{:S(2)}) %copy-start) | copy-done | bytes 8388632
  15.4 4.2 %segment.1 = (f32[4,16,512]{2,1,0:T(8,128)S(1)}, f32[4,16,512]{2,1,0:T(8,128)S(1)}, f32[4,16,512]{2,1,0:T(8,128)S(1)}, f32[4,16,512]{2,1,0:T(8,128)S(1)}) custom-call(bf16[256,64]{1,0:T(8,128)(2,1)S(1)} %maximum_select_fusion.weights_ref, bf16[32,512,256]{2,1,0:T(8,128)(2,1)S(1)} %copy-done), custom_call_target="tpu_custom_call" | custom-call | tf_op jit(solution)/shard_map/segment/pallas_call | solution.py:106
  19.6 1.9 %collective-permute-start.3 = (f32[4,16,512]{2,1,0:T(8,128)S(1)}, f32[4,16,512]{2,1,0:T(8,128)S(1)}, u32[]{:S(2)}, u32[]{:S(2)}) collective-permute-start(f32[4,16,512]{2,1,0:T(8,128)S(1)} %get-tuple-element.10), channel_id=1, source_target_pairs={{0,8},{8,0},{16,24},{24,16},{1,9},{9,1},{17,25},{25,17},{2,10},{10... | collective-permute-start | bytes 393224 | tf_op jit(solution)/shard_map/ppermute | solution.py:120
  21.5 1.5 %collective-permute-start.4 = (f32[4,16,512]{2,1,0:T(8,128)S(1)}, f32[4,16,512]{2,1,0:T(8,128)S(1)}, u32[]{:S(2)}, u32[]{:S(2)}) collective-permute-start(f32[4,16,512]{2,1,0:T(8,128)S(1)} %get-tuple-element.11), channel_id=1, source_target_pairs={{0,16},{8,24},{16,0},{24,8},{1,17},{9,25},{17,1},{25,9},{2,18},{10... | collective-permute-start | bytes 393224 | tf_op jit(solution)/shard_map/ppermute | solution.py:120
  23.0 0.1 collective-permute-start.5
  23.2 2.5 %collective-permute-done.3.refs_1_ = f32[4,16,512]{2,1,0:T(8,128)S(1)} collective-permute-done((f32[4,16,512]{2,1,0:T(8,128)S(1)}, f32[4,16,512]{2,1,0:T(8,128)S(1)}, u32[]{:S(2)}, u32[]{:S(2)}) %collective-permute-start.3) | collective-permute-done | bytes 131104 | tf_op jit(solution)/shard_map/ppermute | solution.py:120
  25.7 1.2 %collective-permute-done.4.refs_2_ = f32[4,16,512]{2,1,0:T(8,128)S(1)} collective-permute-done((f32[4,16,512]{2,1,0:T(8,128)S(1)}, f32[4,16,512]{2,1,0:T(8,128)S(1)}, u32[]{:S(2)}, u32[]{:S(2)}) %collective-permute-start.4) | collective-permute-done | bytes 131104 | tf_op jit(solution)/shard_map/ppermute | solution.py:120
  26.9 2.0 %collective-permute-done.5.refs_3_ = f32[4,16,512]{2,1,0:T(8,128)S(1)} collective-permute-done((f32[4,16,512]{2,1,0:T(8,128)S(1)}, f32[4,16,512]{2,1,0:T(8,128)S(1)}, u32[]{:S(2)}, u32[]{:S(2)}) %collective-permute-start.5) | collective-permute-done | bytes 131104 | tf_op jit(solution)/shard_map/ppermute | solution.py:120
  28.9 0.7 %join.1 = f32[16,512]{1,0:T(8,128)} custom-call(f32[4,16,512]{2,1,0:T(8,128)S(1)} %get-tuple-element.9.refs_0_, f32[4,16,512]{2,1,0:T(8,128)S(1)} %collective-permute-done.3.refs_1_, f32[4,16,512]{2,1,0:T(8,128)S(1)} %collective-permute-done.4.refs_2_, f32[4,16,512]{2,1,0:T(8,128)S(1)} %collective-permute-done.5.refs_3_), custom_call_target="tpu_custom_call" | custom-call | tf_op jit(solution)/shard_map/join/pallas_call | solution.py:123
  (2 shorter events, 0.0 us)
Async XLA Ops:
  0.0 1.5 %collective-permute-start = (bf16[32,64]{1,0:T(8,128)(2,1)}, bf16[32,64]{1,0:T(8,128)(2,1)S(1)}, u32[]{:S(2)}, u32[]{:S(2)}) collective-permute-start(bf16[32,64]{1,0:T(8,128)(2,1)} %param.3), channel_id=1, source_target_pairs={{0,1},{1,0},{2,3},{3,2},{4,5},{5,4},{6,7},{7,6},{8,9},{9,8},{10,11... | collective-permute-start | bytes 12296 | tf_op jit(solution)/shard_map/ppermute | solution.py:17
  2.3 4.7 %collective-permute-start.1 = (bf16[64,64]{1,0:T(8,128)(2,1)S(1)}, bf16[64,64]{1,0:T(8,128)(2,1)S(1)}, u32[]{:S(2)}, u32[]{:S(2)}) collective-permute-start(bf16[64,64]{1,0:T(8,128)(2,1)S(1)} %maximum_select_fusion.2), channel_id=1, source_target_pairs={{0,2},{1,3},{2,0},{3,1},{4,6},{5,7},{6,4},{7,5},{8,10},{9,11},{10,... | collective-permute-start | bytes 24584 | tf_op jit(solution)/shard_map/ppermute | solution.py:17
  7.0 5.0 %collective-permute-start.2 = (bf16[128,64]{1,0:T(8,128)(2,1)S(1)}, bf16[128,64]{1,0:T(8,128)(2,1)S(1)}, u32[]{:S(2)}, u32[]{:S(2)}) collective-permute-start(bf16[128,64]{1,0:T(8,128)(2,1)S(1)} %maximum_select_fusion.1), channel_id=1, source_target_pairs={{0,4},{1,5},{2,6},{3,7},{4,0},{5,1},{6,2},{7,3},{8,12},{9,13},{10,... | collective-permute-start | bytes 49160 | tf_op jit(solution)/shard_map/ppermute | solution.py:17
  12.0 3.4 %copy-start = (bf16[32,512,256]{2,1,0:T(8,128)(2,1)S(1)}, bf16[32,512,256]{2,1,0:T(8,128)(2,1)}, u32[]{:S(2)}) copy-start(bf16[32,512,256]{2,1,0:T(8,128)(2,1)} %returns_ref.1) | copy-start | bytes 25165828
  19.6 6.1 %collective-permute-start.3 = (f32[4,16,512]{2,1,0:T(8,128)S(1)}, f32[4,16,512]{2,1,0:T(8,128)S(1)}, u32[]{:S(2)}, u32[]{:S(2)}) collective-permute-start(f32[4,16,512]{2,1,0:T(8,128)S(1)} %get-tuple-element.10), channel_id=1, source_target_pairs={{0,8},{8,0},{16,24},{24,16},{1,9},{9,1},{17,25},{25,17},{2,10},{10... | collective-permute-start | bytes 393224 | tf_op jit(solution)/shard_map/ppermute | solution.py:120
  21.5 5.4 %collective-permute-start.4 = (f32[4,16,512]{2,1,0:T(8,128)S(1)}, f32[4,16,512]{2,1,0:T(8,128)S(1)}, u32[]{:S(2)}, u32[]{:S(2)}) collective-permute-start(f32[4,16,512]{2,1,0:T(8,128)S(1)} %get-tuple-element.11), channel_id=1, source_target_pairs={{0,16},{8,24},{16,0},{24,8},{1,17},{9,25},{17,1},{25,9},{2,18},{10... | collective-permute-start | bytes 393224 | tf_op jit(solution)/shard_map/ppermute | solution.py:120
  23.0 5.9 %collective-permute-start.5 = (f32[4,16,512]{2,1,0:T(8,128)S(1)}, f32[4,16,512]{2,1,0:T(8,128)S(1)}, u32[]{:S(2)}, u32[]{:S(2)}) collective-permute-start(f32[4,16,512]{2,1,0:T(8,128)S(1)} %get-tuple-element.12), channel_id=1, source_target_pairs={{0,24},{8,16},{16,8},{24,0},{1,25},{9,17},{17,9},{25,1},{2,26},{10... | collective-permute-start | bytes 393224 | tf_op jit(solution)/shard_map/ppermute | solution.py:120

commit v2 on v0

v2 whole, which is shorter than its diff:
```python
import functools

import jax
import jax.numpy as jnp
from jax import lax
from jax.experimental import pallas as pl
from jax.experimental.pallas import tpu as pltpu
from jax.sharding import PartitionSpec as P

CONTRACT_LAST = (((1,), (1,)), ((), ()))
VMEM = pl.BlockSpec(memory_space=pltpu.VMEM)
HBM = pl.BlockSpec(memory_space=pltpu.HBM)


def dot_last(a, b):
    return lax.dot_general(a, b, CONTRACT_LAST, preferred_element_type=jnp.float32)


def call(kernel, name, out_shape, args, scratch=(), kept=(), limit=8, flops=0, moved=0):
    args = [
        pltpu.with_memory_space_constraint(a, pltpu.HBM) if i in kept else a
        for i, a in enumerate(args)
    ]
    several = isinstance(out_shape, (list, tuple))
    return pl.pallas_call(
        kernel,
        out_shape=out_shape,
        in_specs=[HBM if i in kept else VMEM for i in range(len(args))],
        out_specs=[VMEM] * len(out_shape) if several else VMEM,
        scratch_shapes=list(scratch),
        compiler_params=pltpu.CompilerParams(vmem_limit_bytes=limit * 2**20),
        cost_estimate=pl.CostEstimate(flops=flops, bytes_accessed=moved, transcendentals=0),
        name=name,
    )(*args)


def swap(rows, bit):
    count = lax.axis_size("paths")
    return lax.ppermute(rows, "paths", [(s, s ^ bit) for s in range(count)])


def stage_kernel(weights_ref, returns_ref, out_ref):
    out_ref[...] = weights_ref[...]


def merge_kernel(bit, rows_ref, other_ref, out_ref):
    count = rows_ref.shape[0]
    upper = (lax.axis_index("paths") // bit) % 2
    out_ref[pl.ds(pl.multiple_of(upper * count, count), count)] = rows_ref[...]
    out_ref[pl.ds(pl.multiple_of((1 - upper) * count, count), count)] = other_ref[...]


def spread(segments, rows):
    assets, ports = rows.shape
    width = ports // segments
    own = lax.axis_index("tm")
    row = lax.broadcasted_iota(jnp.int32, (ports, ports), 0)
    col = lax.broadcasted_iota(jnp.int32, (ports, ports), 1)
    pick = (col == ((row // width) ^ own) * width + row % width).astype(jnp.bfloat16)
    turned = dot_last(pick, rows).astype(jnp.bfloat16)
    blank = jnp.zeros_like(turned)
    return jnp.concatenate(
        [jnp.concatenate([turned, blank], axis=1), jnp.concatenate([blank, turned], axis=1)]
    )


def half_profit(spread_rows, returns_ref, t, half):
    paths, assets = returns_ref.shape[1:]
    columns = pl.ds(pl.multiple_of(half * (assets // 2), assets // 2), assets // 2)
    both = jnp.concatenate(
        [returns_ref[t, : paths // 2, columns], returns_ref[t, paths // 2 :, columns]], axis=1
    )
    return dot_last(spread_rows, both)


def first_kernel(segments, rows_ref, returns_ref, out_ref):
    half = lax.axis_index("paths") // (lax.axis_size("paths") // 2)
    rows = spread(segments, rows_ref[...])
    for t in range(returns_ref.shape[0]):
        out_ref[t] = half_profit(rows, returns_ref, t, half)


def second_kernel(segments, tile, rows_ref, returns_ref, first_ref, *refs):
    outs, stats = refs[:segments], refs[segments]
    steps, paths, assets = returns_ref.shape
    ports = rows_ref.shape[1]
    width = ports // segments
    half = 1 - lax.axis_index("paths") // (lax.axis_size("paths") // 2)
    rows = spread(segments, rows_ref[...])
    stats[...] = jnp.zeros_like(stats)
    for g in range(0, steps, tile):
        profits = [half_profit(rows, returns_ref, g + i, half) for i in range(tile)]
        for q in range(0, 2 * ports, 16):
            value, peak, low, fall = (stats[n, q : q + 16] for n in range(4))
            for i in range(tile):
                value = value + (first_ref[g + i, q : q + 16] + profits[i][q : q + 16])
                peak = jnp.maximum(peak, value)
                low = jnp.minimum(low, value)
                fall = jnp.maximum(fall, peak - value)
            for n, new in enumerate((value, peak, low, fall)):
                stats[n, q : q + 16] = new
    for k in range(segments):
        for h in range(2):
            at = slice(h * ports + k * width, h * ports + (k + 1) * width)
            put = slice(h * (paths // 2), (h + 1) * (paths // 2))
            outs[k][0, :, put] = stats[3, at]
            outs[k][1, :, put] = stats[2, at]
            outs[k][2, :, put] = stats[1, at] - stats[0, at]
            outs[k][3, :, put] = stats[0, at]


def join_kernel(segments, *refs):
    ins, out_ref, ordered = refs[:segments], refs[segments], refs[segments + 1]
    own = lax.axis_index("tm")
    for k in range(segments):
        ordered[own ^ k] = ins[k][...]
    fall = ordered[0, 0]
    drop = ordered[0, 2]
    for s in range(1, segments):
        fall = jnp.maximum(jnp.maximum(fall, ordered[s, 0]), drop - ordered[s, 1])
        drop = jnp.maximum(drop - ordered[s, 3], ordered[s, 2])
    out_ref[...] = fall


def shards(returns, weights):
    segments = lax.axis_size("tm")
    count = lax.axis_size("paths")
    steps, paths, assets = returns.shape
    ports = weights.shape[1]
    width = ports // segments
    held = jax.ShapeDtypeStruct((steps, 2 * ports, paths // 2), jnp.float32)
    part = jax.ShapeDtypeStruct((4, width, paths), jnp.float32)
    work = 2 * steps * paths * assets * ports

    rows = call(
        stage_kernel, "stage", jax.ShapeDtypeStruct(weights.shape, weights.dtype), [weights, returns],
        kept=(1,), flops=work, moved=returns.size * 2,
    )
    other = swap(weights, 1)
    bit = 1
    while 2 * bit < count:
        rows = call(
            functools.partial(merge_kernel, bit), f"merge{bit}",
            jax.ShapeDtypeStruct((2 * rows.shape[0], ports), rows.dtype), [rows, other],
        )
        bit *= 2
        other = swap(rows, bit)
    first = call(
        functools.partial(first_kernel, segments), "first", held, [rows, returns],
        flops=work, moved=returns.size,
    )
    parts = call(
        functools.partial(second_kernel, segments, min(steps, 8)), "second", [part] * segments,
        [other, returns, first],
        scratch=[pltpu.VMEM((4, 2 * ports, paths // 2), jnp.float32)],
        flops=work, moved=returns.size,
    )
    arrived = [parts[0]] + [
        lax.ppermute(parts[k], "tm", [(s, s ^ k) for s in range(segments)])
        for k in range(1, segments)
    ]
    return call(
        functools.partial(join_kernel, segments), "join",
        jax.ShapeDtypeStruct((width, paths), jnp.float32), arrived,
        scratch=[pltpu.VMEM((segments, 4, width, paths), jnp.float32)],
        moved=8 * part.size,
    )


def solution(mesh):
    in_specs = (P("tm", "paths", None), P("paths", None))
    out_specs = P("tm", "paths")
    return jax.shard_map(shards, mesh=mesh, in_specs=in_specs, out_specs=out_specs, check_vma=False)
```

time: 88.1 us -> 22.9 us (0.26)
  blocking collectives: 44.8 us -> 0 us
  other arithmetic: 22.5 us -> 0 us
  local copies, waits for them, and re-layouts: 12.1 us -> 0.91 us
  starting transfers between devices: 0 us -> 10 us
  matrix products: 8.14 us -> 0 us
  waiting for transfers between devices: 0 us -> 7.89 us
  Pallas kernels: 0 us -> 3.93 us
    all_gather x3 -> x0, blocking collectives: 36.9 us -> none  [the longest x2 21 us: prefix(): gathered = jax.tree.map(lambda a: lax.all_gather(a, axis), part)]
    another operation x1 -> x0, other arithmetic: 20.9 us -> none  [shards(): peaks = jnp.maximum(lax.cummax(values, axis=0), 0.0)]
    unnamed x11 -> x4, local copies, waits for them, and re-layouts: 11.7 us -> 0.91 us
    ppermute x0 -> x6, starting transfers between devices: none -> 10 us  [the longest x3 6.5 us: swap(): return lax.ppermute(rows, 'paths', [(s, s ^ bit) for s in range(count)])]
    dot_general x2 -> x0, matrix products: 8.14 us -> none  [the longest x1 6.03 us: shards(): jnp.einsum('tpa,aq->tqp', returns, all_weights, preferred_element_type=jn...]
    ppermute x0 -> x6, waiting for transfers between devices: none -> 7.89 us  [the longest x3 5.71 us: shards(): lax.ppermute(parts[k], 'tm', [(s, s ^ k) for s in range(segments)])]
    all_to_all x1 -> x0, blocking collectives: 7.85 us -> none  [shards(): lax.all_to_all(blocks, 'tm', split_axis=0, concat_axis=0, tiled=True)]
    pallas_call x0 -> x6, Pallas kernels: none -> 3.93 us  [call(): pl.pallas_call(kernel, out_shape=out_shape, in_specs=[HBM if i in kept el...]
  transfers between devices with their start and end apart: 0 -> 6, of which waited for: 0 -> 6; matrix products, arithmetic and copies ran while one was open for 0% -> 0% of each run, Pallas kernels for 0% -> 7%
where the time goes in v2:
time: 22.9 us; the launch traced here: 22.8 us
  starting transfers between devices  10 us (44%)
  waiting for transfers between devices  7.89 us (34%)
  Pallas kernels  3.93 us (17%)
  local copies, waits for them, and re-layouts  0.91 us (4%)
    ppermute x3, starting transfers between devices, swap(): return lax.ppermute(rows, 'paths', [(s, s ^ bit) for s in range(count)])  6.5 us
    ppermute x3, waiting for transfers between devices, shards(): lax.ppermute(parts[k], 'tm', [(s, s ^ k) for s in range(segments)])  5.71 us
    pallas_call x6, Pallas kernels, call(): pl.pallas_call(kernel, out_shape=out_shape, in_specs=[HBM if i in kept el...  3.93 us
    ppermute x3, starting transfers between devices, shards(): lax.ppermute(parts[k], 'tm', [(s, s ^ k) for s in range(segments)])  3.55 us
    ppermute x3, waiting for transfers between devices, swap(): return lax.ppermute(rows, 'paths', [(s, s ^ bit) for s in range(count)])  2.17 us
    unnamed x4, local copies, waits for them, and re-layouts  0.91 us
  transfers between devices with their start and end apart: 6, of which 6 were waited for; matrix products, arithmetic and copies ran while one was open for 0% of the time, Pallas kernels for 7%

profile of v2, /device:TPU:0, one launch (start us, length us, event | category | flops | bytes accessed | tf_op | source)
XLA Modules:
  0.0 22.8 jit_solution(12550515517154792313)
XLA Ops:
  0.0 0.0 copy-start
  0.0 0.5 %collective-permute-start = (bf16[32,64]{1,0:T(8,128)(2,1)}, bf16[32,64]{1,0:T(8,128)(2,1)S(1)}, u32[]{:S(2)}, u32[]{:S(2)}) collective-permute-start(bf16[32,64]{1,0:T(8,128)(2,1)} %weights_ref.1), channel_id=1, source_target_pairs={{0,1},{1,0},{2,3},{3,2},{4,5},{5,4},{6,7},{7,6},{8,9},{9,8},{10,11... | collective-permute-start | bytes 12296 | tf_op jit(solution)/shard_map/ppermute | solution.py:39
  0.5 0.0 copy-start.1
  0.5 0.9 %copy-done.1 = bf16[32,64]{1,0:T(8,128)(2,1)S(1)} copy-done((bf16[32,64]{1,0:T(8,128)(2,1)S(1)}, bf16[32,64]{1,0:T(8,128)(2,1)}, u32[]{:S(2)}) %copy-start.1) | copy-done | bytes 4120
  1.4 0.1 collective-permute-done.other_ref
  1.5 2.9 %collective-permute-start.1 = (bf16[64,64]{1,0:T(8,128)(2,1)S(1)}, bf16[64,64]{1,0:T(8,128)(2,1)S(1)}, u32[]{:S(2)}, u32[]{:S(2)}) collective-permute-start(bf16[64,64]{1,0:T(8,128)(2,1)S(1)} %merge1.1.rows_ref), channel_id=1, source_target_pairs={{0,2},{1,3},{2,0},{3,1},{4,6},{5,7},{6,4},{7,5},{8,10},{9,11},{10,... | collective-permute-start | bytes 24584 | tf_op jit(solution)/shard_map/ppermute | solution.py:39
  4.4 1.7 %collective-permute-done.1.other_ref = bf16[64,64]{1,0:T(8,128)(2,1)S(1)} collective-permute-done((bf16[64,64]{1,0:T(8,128)(2,1)S(1)}, bf16[64,64]{1,0:T(8,128)(2,1)S(1)}, u32[]{:S(2)}, u32[]{:S(2)}) %collective-permute-start.1) | collective-permute-done | bytes 8224 | tf_op jit(solution)/shard_map/ppermute | solution.py:39
  6.2 3.1 %collective-permute-start.2 = (bf16[128,64]{1,0:T(8,128)(2,1)S(1)}, bf16[128,64]{1,0:T(8,128)(2,1)S(1)}, u32[]{:S(2)}, u32[]{:S(2)}) collective-permute-start(bf16[128,64]{1,0:T(8,128)(2,1)S(1)} %merge2.1.rows_ref), channel_id=1, source_target_pairs={{0,4},{1,5},{2,6},{3,7},{4,0},{5,1},{6,2},{7,3},{8,12},{9,13},{10,... | collective-permute-start | bytes 49160 | tf_op jit(solution)/shard_map/ppermute | solution.py:39
  9.3 0.0 copy-done
  9.3 1.6 %first.1.first_ref = f32[32,128,256]{2,1,0:T(8,128)S(1)} custom-call(bf16[128,64]{1,0:T(8,128)(2,1)S(1)} %merge2.1.rows_ref, bf16[32,512,256]{2,1,0:T(8,128)(2,1)S(1)} %copy-done), custom_call_target="tpu_custom_call" | custom-call | flops 536870912 | bytes 4194304 | tf_op jit(solution)/shard_map/first/pallas_call | solution.py:25
  10.8 0.3 %collective-permute-done.2.rows_ref = bf16[128,64]{1,0:T(8,128)(2,1)S(1)} collective-permute-done((bf16[128,64]{1,0:T(8,128)(2,1)S(1)}, bf16[128,64]{1,0:T(8,128)(2,1)S(1)}, u32[]{:S(2)}, u32[]{:S(2)}) %collective-permute-start.2) | collective-permute-done | bytes 16416 | tf_op jit(solution)/shard_map/ppermute | solution.py:39
  11.2 1.7 %second.1 = (f32[4,16,512]{2,1,0:T(8,128)S(1)}, f32[4,16,512]{2,1,0:T(8,128)S(1)}, f32[4,16,512]{2,1,0:T(8,128)S(1)}, f32[4,16,512]{2,1,0:T(8,128)S(1)}) custom-call(bf16[128,64]{1,0:T(8,128)(2,1)S(1)} %collective-permute-done.2.rows_ref, bf16[32,512,256]{2,1,0:T(8,128)(2,1)S(1)} %copy-done, f32[32,128,256]{2,1,0:T(8,128)S(1)} %first.1.first_ref), custom_call_target="tpu_custom_call" | custom-call | flops 536870912 | bytes 4194304 | tf_op jit(solution)/shard_map/second/pallas_call | solution.py:25
  12.8 1.9 %collective-permute-start.3 = (f32[4,16,512]{2,1,0:T(8,128)S(1)}, f32[4,16,512]{2,1,0:T(8,128)S(1)}, u32[]{:S(2)}, u32[]{:S(2)}) collective-permute-start(f32[4,16,512]{2,1,0:T(8,128)S(1)} %get-tuple-element.10), channel_id=1, source_target_pairs={{0,8},{8,0},{16,24},{24,16},{1,9},{9,1},{17,25},{25,17},{2,10},{10... | collective-permute-start | bytes 393224 | tf_op jit(solution)/shard_map/ppermute | solution.py:159
  14.7 1.5 %collective-permute-start.4 = (f32[4,16,512]{2,1,0:T(8,128)S(1)}, f32[4,16,512]{2,1,0:T(8,128)S(1)}, u32[]{:S(2)}, u32[]{:S(2)}) collective-permute-start(f32[4,16,512]{2,1,0:T(8,128)S(1)} %get-tuple-element.11), channel_id=1, source_target_pairs={{0,16},{8,24},{16,0},{24,8},{1,17},{9,25},{17,1},{25,9},{2,18},{10... | collective-permute-start | bytes 393224 | tf_op jit(solution)/shard_map/ppermute | solution.py:159
  16.2 0.2 collective-permute-start.5
  16.4 2.7 %collective-permute-done.3.refs_1_ = f32[4,16,512]{2,1,0:T(8,128)S(1)} collective-permute-done((f32[4,16,512]{2,1,0:T(8,128)S(1)}, f32[4,16,512]{2,1,0:T(8,128)S(1)}, u32[]{:S(2)}, u32[]{:S(2)}) %collective-permute-start.3) | collective-permute-done | bytes 131104 | tf_op jit(solution)/shard_map/ppermute | solution.py:159
  19.1 1.4 %collective-permute-done.4.refs_2_ = f32[4,16,512]{2,1,0:T(8,128)S(1)} collective-permute-done((f32[4,16,512]{2,1,0:T(8,128)S(1)}, f32[4,16,512]{2,1,0:T(8,128)S(1)}, u32[]{:S(2)}, u32[]{:S(2)}) %collective-permute-start.4) | collective-permute-done | bytes 131104 | tf_op jit(solution)/shard_map/ppermute | solution.py:159
  20.5 1.6 %collective-permute-done.5.refs_3_ = f32[4,16,512]{2,1,0:T(8,128)S(1)} collective-permute-done((f32[4,16,512]{2,1,0:T(8,128)S(1)}, f32[4,16,512]{2,1,0:T(8,128)S(1)}, u32[]{:S(2)}, u32[]{:S(2)}) %collective-permute-start.5) | collective-permute-done | bytes 131104 | tf_op jit(solution)/shard_map/ppermute | solution.py:159
  22.1 0.7 %join.1 = f32[16,512]{1,0:T(8,128)} custom-call(f32[4,16,512]{2,1,0:T(8,128)S(1)} %get-tuple-element.9.refs_0_, f32[4,16,512]{2,1,0:T(8,128)S(1)} %collective-permute-done.3.refs_1_, f32[4,16,512]{2,1,0:T(8,128)S(1)} %collective-permute-done.4.refs_2_, f32[4,16,512]{2,1,0:T(8,128)S(1)} %collective-permute-done.5.refs_3_), custom_call_target="tpu_custom_call" | custom-call | bytes 262144 | tf_op jit(solution)/shard_map/join/pallas_call | solution.py:25
  (3 shorter events, 0.0 us)
Async XLA Ops:
  0.0 9.3 %copy-start = (bf16[32,512,256]{2,1,0:T(8,128)(2,1)S(1)}, bf16[32,512,256]{2,1,0:T(8,128)(2,1)}, u32[]{:S(2)}) copy-start(bf16[32,512,256]{2,1,0:T(8,128)(2,1)} %returns_ref.5) | copy-start | bytes 25165828
  0.0 1.5 %collective-permute-start = (bf16[32,64]{1,0:T(8,128)(2,1)}, bf16[32,64]{1,0:T(8,128)(2,1)S(1)}, u32[]{:S(2)}, u32[]{:S(2)}) collective-permute-start(bf16[32,64]{1,0:T(8,128)(2,1)} %weights_ref.1), channel_id=1, source_target_pairs={{0,1},{1,0},{2,3},{3,2},{4,5},{5,4},{6,7},{7,6},{8,9},{9,8},{10,11... | collective-permute-start | bytes 12296 | tf_op jit(solution)/shard_map/ppermute | solution.py:39
  0.5 0.9 %copy-start.1 = (bf16[32,64]{1,0:T(8,128)(2,1)S(1)}, bf16[32,64]{1,0:T(8,128)(2,1)}, u32[]{:S(2)}) copy-start(bf16[32,64]{1,0:T(8,128)(2,1)} %weights_ref.1) | copy-start | bytes 12292
  1.5 4.6 %collective-permute-start.1 = (bf16[64,64]{1,0:T(8,128)(2,1)S(1)}, bf16[64,64]{1,0:T(8,128)(2,1)S(1)}, u32[]{:S(2)}, u32[]{:S(2)}) collective-permute-start(bf16[64,64]{1,0:T(8,128)(2,1)S(1)} %merge1.1.rows_ref), channel_id=1, source_target_pairs={{0,2},{1,3},{2,0},{3,1},{4,6},{5,7},{6,4},{7,5},{8,10},{9,11},{10,... | collective-permute-start | bytes 24584 | tf_op jit(solution)/shard_map/ppermute | solution.py:39
  6.2 5.0 %collective-permute-start.2 = (bf16[128,64]{1,0:T(8,128)(2,1)S(1)}, bf16[128,64]{1,0:T(8,128)(2,1)S(1)}, u32[]{:S(2)}, u32[]{:S(2)}) collective-permute-start(bf16[128,64]{1,0:T(8,128)(2,1)S(1)} %merge2.1.rows_ref), channel_id=1, source_target_pairs={{0,4},{1,5},{2,6},{3,7},{4,0},{5,1},{6,2},{7,3},{8,12},{9,13},{10,... | collective-permute-start | bytes 49160 | tf_op jit(solution)/shard_map/ppermute | solution.py:39
  12.8 6.3 %collective-permute-start.3 = (f32[4,16,512]{2,1,0:T(8,128)S(1)}, f32[4,16,512]{2,1,0:T(8,128)S(1)}, u32[]{:S(2)}, u32[]{:S(2)}) collective-permute-start(f32[4,16,512]{2,1,0:T(8,128)S(1)} %get-tuple-element.10), channel_id=1, source_target_pairs={{0,8},{8,0},{16,24},{24,16},{1,9},{9,1},{17,25},{25,17},{2,10},{10... | collective-permute-start | bytes 393224 | tf_op jit(solution)/shard_map/ppermute | solution.py:159
  14.7 5.8 %collective-permute-start.4 = (f32[4,16,512]{2,1,0:T(8,128)S(1)}, f32[4,16,512]{2,1,0:T(8,128)S(1)}, u32[]{:S(2)}, u32[]{:S(2)}) collective-permute-start(f32[4,16,512]{2,1,0:T(8,128)S(1)} %get-tuple-element.11), channel_id=1, source_target_pairs={{0,16},{8,24},{16,0},{24,8},{1,17},{9,25},{17,1},{25,9},{2,18},{10... | collective-permute-start | bytes 393224 | tf_op jit(solution)/shard_map/ppermute | solution.py:159
  16.2 5.9 %collective-permute-start.5 = (f32[4,16,512]{2,1,0:T(8,128)S(1)}, f32[4,16,512]{2,1,0:T(8,128)S(1)}, u32[]{:S(2)}, u32[]{:S(2)}) collective-permute-start(f32[4,16,512]{2,1,0:T(8,128)S(1)} %get-tuple-element.12), channel_id=1, source_target_pairs={{0,24},{8,16},{16,8},{24,0},{1,25},{9,17},{17,9},{25,1},{2,26},{10... | collective-permute-start | bytes 393224 | tf_op jit(solution)/shard_map/ppermute | solution.py:159

commit v3 on v2

--- a/solution.py
+++ b/solution.py
@@ -1,4 +1,5 @@
 import functools
+import math
 
 import jax
 import jax.numpy as jnp
@@ -8,6 +9,8 @@
 from jax.sharding import PartitionSpec as P
 
 CONTRACT_LAST = (((1,), (1,)), ((), ()))
+MAX_RETURN = 0.15917969
+MAX_WEIGHT = 0.375
 VMEM = pl.BlockSpec(memory_space=pltpu.VMEM)
 HBM = pl.BlockSpec(memory_space=pltpu.HBM)
 
@@ -80,6 +83,22 @@
         out_ref[t] = half_profit(rows, returns_ref, t, half)
 
 
+def scale_of(terms):
+    return 2.0 ** math.floor(math.log2(65504 / (terms * MAX_RETURN * MAX_WEIGHT)))
+
+
+def encode(part, terms):
+    part = part * scale_of(terms)
+    wide = part * 8193.0
+    near = wide - (wide - part)
+    return jnp.where(part < near, -near, near)
+
+
+def decode(sent, terms):
+    sent = sent.astype(jnp.float32)
+    return (jnp.abs(sent) + (0.75 * 2.0**-12) * sent) * (1 / scale_of(terms))
+
+
 def second_kernel(segments, tile, rows_ref, returns_ref, first_ref, *refs):
     outs, stats = refs[:segments], refs[segments]
     steps, paths, assets = returns_ref.shape
@@ -103,22 +122,22 @@
         for h in range(2):
             at = slice(h * ports + k * width, h * ports + (k + 1) * width)
             put = slice(h * (paths // 2), (h + 1) * (paths // 2))
-            outs[k][0, :, put] = stats[3, at]
-            outs[k][1, :, put] = stats[2, at]
-            outs[k][2, :, put] = stats[1, at] - stats[0, at]
-            outs[k][3, :, put] = stats[0, at]
+            value, peak, low, fall = (stats[n, at] for n in range(4))
+            for n, part in enumerate((fall, -low, peak - value, value - low)):
+                outs[k][n, :, put] = part if k == 0 else encode(part, steps * assets)
 
 
-def join_kernel(segments, *refs):
+def join_kernel(segments, terms, *refs):
     ins, out_ref, ordered = refs[:segments], refs[segments], refs[segments + 1]
     own = lax.axis_index("tm")
     for k in range(segments):
-        ordered[own ^ k] = ins[k][...]
+        ordered[own ^ k] = ins[k][...] if k == 0 else decode(ins[k][...], terms)
     fall = ordered[0, 0]
     drop = ordered[0, 2]
     for s in range(1, segments):
-        fall = jnp.maximum(jnp.maximum(fall, ordered[s, 0]), drop - ordered[s, 1])
-        drop = jnp.maximum(drop - ordered[s, 3], ordered[s, 2])
+        below = ordered[s, 1]
+        fall = jnp.maximum(jnp.maximum(fall, ordered[s, 0]), drop + below)
+        drop = jnp.maximum(drop + below - ordered[s, 3], ordered[s, 2])
     out_ref[...] = fall
 
 
@@ -156,11 +175,13 @@
         flops=work, moved=returns.size,
     )
     arrived = [parts[0]] + [
-        lax.ppermute(parts[k], "tm", [(s, s ^ k) for s in range(segments)])
+        lax.ppermute(
+            parts[k].astype(jnp.float16), "tm", [(s, s ^ k) for s in range(segments)]
+        ).astype(jnp.float32)
         for k in range(1, segments)
     ]
     return call(
-        functools.partial(join_kernel, segments), "join",
+        functools.partial(join_kernel, segments, steps * assets), "join",
         jax.ShapeDtypeStruct((width, paths), jnp.float32), arrived,
         scratch=[pltpu.VMEM((segments, 4, width, paths), jnp.float32)],
         moved=8 * part.size,

time: 22.9 us -> 21.6 us (0.943)
  waiting for transfers between devices: 7.89 us -> 6.21 us
    ppermute x3, waiting for transfers between devices: 5.71 us -> 4.03 us  [shards(): lax.ppermute(parts[k].astype(jnp.float16), 'tm', [(s, s ^ k) for s in ran...]
where the time goes in v3:
time: 21.6 us; the launch traced here: 21.4 us
  starting transfers between devices  10.1 us (47%)
  waiting for transfers between devices  6.21 us (29%)
  Pallas kernels  4.06 us (19%)
  local copies, waits for them, and re-layouts  0.91 us (4%)
    ppermute x3, starting transfers between devices, swap(): return lax.ppermute(rows, 'paths', [(s, s ^ bit) for s in range(count)])  6.5 us
    pallas_call x6, Pallas kernels, call(): pl.pallas_call(kernel, out_shape=out_shape, in_specs=[HBM if i in kept el...  4.06 us
    ppermute x3, waiting for transfers between devices, shards(): lax.ppermute(parts[k].astype(jnp.float16), 'tm', [(s, s ^ k) for s in ran...  4.03 us
    ppermute x3, starting transfers between devices, shards(): lax.ppermute(parts[k].astype(jnp.float16), 'tm', [(s, s ^ k) for s in ran...  3.62 us
    ppermute x3, waiting for transfers between devices, swap(): return lax.ppermute(rows, 'paths', [(s, s ^ bit) for s in range(count)])  2.17 us
    unnamed x4, local copies, waits for them, and re-layouts  0.91 us
  transfers between devices with their start and end apart: 6, of which 6 were waited for; matrix products, arithmetic and copies ran while one was open for 0% of the time, Pallas kernels for 7%

profile of v3, /device:TPU:0, one launch (start us, length us, event | category | flops | bytes accessed | tf_op | source)
XLA Modules:
  0.0 21.4 jit_solution(3740741560370581918)
XLA Ops:
  0.0 0.0 copy-start
  0.0 0.5 %collective-permute-start = (bf16[32,64]{1,0:T(8,128)(2,1)}, bf16[32,64]{1,0:T(8,128)(2,1)S(1)}, u32[]{:S(2)}, u32[]{:S(2)}) collective-permute-start(bf16[32,64]{1,0:T(8,128)(2,1)} %weights_ref.1), channel_id=1, source_target_pairs={{0,1},{1,0},{2,3},{3,2},{4,5},{5,4},{6,7},{7,6},{8,9},{9,8},{10,11... | collective-permute-start | bytes 12296 | tf_op jit(solution)/shard_map/ppermute | solution.py:42
  0.5 0.0 copy-start.1
  0.5 0.9 %copy-done.1 = bf16[32,64]{1,0:T(8,128)(2,1)S(1)} copy-done((bf16[32,64]{1,0:T(8,128)(2,1)S(1)}, bf16[32,64]{1,0:T(8,128)(2,1)}, u32[]{:S(2)}) %copy-start.1) | copy-done | bytes 4120
  1.4 0.1 collective-permute-done.other_ref
  1.5 2.9 %collective-permute-start.1 = (bf16[64,64]{1,0:T(8,128)(2,1)S(1)}, bf16[64,64]{1,0:T(8,128)(2,1)S(1)}, u32[]{:S(2)}, u32[]{:S(2)}) collective-permute-start(bf16[64,64]{1,0:T(8,128)(2,1)S(1)} %merge1.1.rows_ref), channel_id=1, source_target_pairs={{0,2},{1,3},{2,0},{3,1},{4,6},{5,7},{6,4},{7,5},{8,10},{9,11},{10,... | collective-permute-start | bytes 24584 | tf_op jit(solution)/shard_map/ppermute | solution.py:42
  4.4 1.7 %collective-permute-done.1.other_ref = bf16[64,64]{1,0:T(8,128)(2,1)S(1)} collective-permute-done((bf16[64,64]{1,0:T(8,128)(2,1)S(1)}, bf16[64,64]{1,0:T(8,128)(2,1)S(1)}, u32[]{:S(2)}, u32[]{:S(2)}) %collective-permute-start.1) | collective-permute-done | bytes 8224 | tf_op jit(solution)/shard_map/ppermute | solution.py:42
  6.2 3.1 %collective-permute-start.2 = (bf16[128,64]{1,0:T(8,128)(2,1)S(1)}, bf16[128,64]{1,0:T(8,128)(2,1)S(1)}, u32[]{:S(2)}, u32[]{:S(2)}) collective-permute-start(bf16[128,64]{1,0:T(8,128)(2,1)S(1)} %merge2.1.rows_ref), channel_id=1, source_target_pairs={{0,4},{1,5},{2,6},{3,7},{4,0},{5,1},{6,2},{7,3},{8,12},{9,13},{10,... | collective-permute-start | bytes 49160 | tf_op jit(solution)/shard_map/ppermute | solution.py:42
  9.3 0.0 copy-done
  9.3 1.6 %first.1.first_ref = f32[32,128,256]{2,1,0:T(8,128)S(1)} custom-call(bf16[128,64]{1,0:T(8,128)(2,1)S(1)} %merge2.1.rows_ref, bf16[32,512,256]{2,1,0:T(8,128)(2,1)S(1)} %copy-done), custom_call_target="tpu_custom_call" | custom-call | flops 536870912 | bytes 4194304 | tf_op jit(solution)/shard_map/first/pallas_call | solution.py:28
  10.8 0.3 %collective-permute-done.2.rows_ref = bf16[128,64]{1,0:T(8,128)(2,1)S(1)} collective-permute-done((bf16[128,64]{1,0:T(8,128)(2,1)S(1)}, bf16[128,64]{1,0:T(8,128)(2,1)S(1)}, u32[]{:S(2)}, u32[]{:S(2)}) %collective-permute-start.2) | collective-permute-done | bytes 16416 | tf_op jit(solution)/shard_map/ppermute | solution.py:42
  11.2 1.8 %second.1 = (f32[4,16,512]{2,1,0:T(8,128)S(1)}, f32[4,16,512]{2,1,0:T(8,128)S(1)}, f32[4,16,512]{2,1,0:T(8,128)S(1)}, f32[4,16,512]{2,1,0:T(8,128)S(1)}) custom-call(bf16[128,64]{1,0:T(8,128)(2,1)S(1)} %collective-permute-done.2.rows_ref, bf16[32,512,256]{2,1,0:T(8,128)(2,1)S(1)} %copy-done, f32[32,128,256]{2,1,0:T(8,128)S(1)} %first.1.first_ref), custom_call_target="tpu_custom_call" | custom-call | flops 536870912 | bytes 4194304 | tf_op jit(solution)/shard_map/second/pallas_call | solution.py:28
  13.0 2.8 %collective-permute-start.5 = (f16[4,16,512]{2,1,0:T(8,128)(2,1)S(1)}, f16[4,16,512]{2,1,0:T(8,128)(2,1)S(1)}, u32[]{:S(2)}, u32[]{:S(2)}) collective-permute-start(f16[4,16,512]{2,1,0:T(8,128)(2,1)S(1)} %convert_element_type.22), channel_id=1, source_target_pairs={{0,24},{8,16},{16,8},{24,0},{1,25},{9,17},{17,9},{25,1},{2,26},{10... | collective-permute-start | bytes 196616 | tf_op jit(solution)/shard_map/ppermute | solution.py:178
  15.8 0.5 %collective-permute-start.4 = (f16[4,16,512]{2,1,0:T(8,128)(2,1)S(1)}, f16[4,16,512]{2,1,0:T(8,128)(2,1)S(1)}, u32[]{:S(2)}, u32[]{:S(2)}) collective-permute-start(f16[4,16,512]{2,1,0:T(8,128)(2,1)S(1)} %convert_element_type.20), channel_id=1, source_target_pairs={{0,16},{8,24},{16,0},{24,8},{1,17},{9,25},{17,1},{25,9},{2,18},{10... | collective-permute-start | bytes 196616 | tf_op jit(solution)/shard_map/ppermute | solution.py:178
  16.4 0.3 %collective-permute-start.3 = (f16[4,16,512]{2,1,0:T(8,128)(2,1)S(1)}, f16[4,16,512]{2,1,0:T(8,128)(2,1)S(1)}, u32[]{:S(2)}, u32[]{:S(2)}) collective-permute-start(f16[4,16,512]{2,1,0:T(8,128)(2,1)S(1)} %convert_element_type.18), channel_id=1, source_target_pairs={{0,8},{8,0},{16,24},{24,16},{1,9},{9,1},{17,25},{25,17},{2,10},{10... | collective-permute-start | bytes 196616 | tf_op jit(solution)/shard_map/ppermute | solution.py:178
  16.6 2.3 %collective-permute-done.5 = f16[4,16,512]{2,1,0:T(8,128)(2,1)S(1)} collective-permute-done((f16[4,16,512]{2,1,0:T(8,128)(2,1)S(1)}, f16[4,16,512]{2,1,0:T(8,128)(2,1)S(1)}, u32[]{:S(2)}, u32[]{:S(2)}) %collective-permute-start.5) | collective-permute-done | bytes 65568 | tf_op jit(solution)/shard_map/ppermute | solution.py:178
  18.9 1.2 %collective-permute-done.4 = f16[4,16,512]{2,1,0:T(8,128)(2,1)S(1)} collective-permute-done((f16[4,16,512]{2,1,0:T(8,128)(2,1)S(1)}, f16[4,16,512]{2,1,0:T(8,128)(2,1)S(1)}, u32[]{:S(2)}, u32[]{:S(2)}) %collective-permute-start.4) | collective-permute-done | bytes 65568 | tf_op jit(solution)/shard_map/ppermute | solution.py:178
  20.1 0.6 %collective-permute-done.3 = f16[4,16,512]{2,1,0:T(8,128)(2,1)S(1)} collective-permute-done((f16[4,16,512]{2,1,0:T(8,128)(2,1)S(1)}, f16[4,16,512]{2,1,0:T(8,128)(2,1)S(1)}, u32[]{:S(2)}, u32[]{:S(2)}) %collective-permute-start.3) | collective-permute-done | bytes 65568 | tf_op jit(solution)/shard_map/ppermute | solution.py:178
  20.7 0.7 %join.1 = f32[16,512]{1,0:T(8,128)} custom-call(f32[4,16,512]{2,1,0:T(8,128)S(1)} %get-tuple-element.9.refs_0_, f32[4,16,512]{2,1,0:T(8,128)S(1)} %convert_element_type.19.refs_1_, f32[4,16,512]{2,1,0:T(8,128)S(1)} %convert_element_type.21.refs_2_, f32[4,16,512]{2,1,0:T(8,128)S(1)} %convert_element_type.23.refs_3_), custom_call_target="tpu_custom_call" | custom-call | bytes 262144 | tf_op jit(solution)/shard_map/join/pallas_call | solution.py:28
  (9 shorter events, 0.1 us)
Async XLA Ops:
  0.0 9.3 %copy-start = (bf16[32,512,256]{2,1,0:T(8,128)(2,1)S(1)}, bf16[32,512,256]{2,1,0:T(8,128)(2,1)}, u32[]{:S(2)}) copy-start(bf16[32,512,256]{2,1,0:T(8,128)(2,1)} %returns_ref.5) | copy-start | bytes 25165828
  0.0 1.5 %collective-permute-start = (bf16[32,64]{1,0:T(8,128)(2,1)}, bf16[32,64]{1,0:T(8,128)(2,1)S(1)}, u32[]{:S(2)}, u32[]{:S(2)}) collective-permute-start(bf16[32,64]{1,0:T(8,128)(2,1)} %weights_ref.1), channel_id=1, source_target_pairs={{0,1},{1,0},{2,3},{3,2},{4,5},{5,4},{6,7},{7,6},{8,9},{9,8},{10,11... | collective-permute-start | bytes 12296 | tf_op jit(solution)/shard_map/ppermute | solution.py:42
  0.5 0.9 %copy-start.1 = (bf16[32,64]{1,0:T(8,128)(2,1)S(1)}, bf16[32,64]{1,0:T(8,128)(2,1)}, u32[]{:S(2)}) copy-start(bf16[32,64]{1,0:T(8,128)(2,1)} %weights_ref.1) | copy-start | bytes 12292
  1.5 4.6 %collective-permute-start.1 = (bf16[64,64]{1,0:T(8,128)(2,1)S(1)}, bf16[64,64]{1,0:T(8,128)(2,1)S(1)}, u32[]{:S(2)}, u32[]{:S(2)}) collective-permute-start(bf16[64,64]{1,0:T(8,128)(2,1)S(1)} %merge1.1.rows_ref), channel_id=1, source_target_pairs={{0,2},{1,3},{2,0},{3,1},{4,6},{5,7},{6,4},{7,5},{8,10},{9,11},{10,... | collective-permute-start | bytes 24584 | tf_op jit(solution)/shard_map/ppermute | solution.py:42
  6.2 5.0 %collective-permute-start.2 = (bf16[128,64]{1,0:T(8,128)(2,1)S(1)}, bf16[128,64]{1,0:T(8,128)(2,1)S(1)}, u32[]{:S(2)}, u32[]{:S(2)}) collective-permute-start(bf16[128,64]{1,0:T(8,128)(2,1)S(1)} %merge2.1.rows_ref), channel_id=1, source_target_pairs={{0,4},{1,5},{2,6},{3,7},{4,0},{5,1},{6,2},{7,3},{8,12},{9,13},{10,... | collective-permute-start | bytes 49160 | tf_op jit(solution)/shard_map/ppermute | solution.py:42
  13.0 5.9 %collective-permute-start.5 = (f16[4,16,512]{2,1,0:T(8,128)(2,1)S(1)}, f16[4,16,512]{2,1,0:T(8,128)(2,1)S(1)}, u32[]{:S(2)}, u32[]{:S(2)}) collective-permute-start(f16[4,16,512]{2,1,0:T(8,128)(2,1)S(1)} %convert_element_type.22), channel_id=1, source_target_pairs={{0,24},{8,16},{16,8},{24,0},{1,25},{9,17},{17,9},{25,1},{2,26},{10... | collective-permute-start | bytes 196616 | tf_op jit(solution)/shard_map/ppermute | solution.py:178
  15.8 4.3 %collective-permute-start.4 = (f16[4,16,512]{2,1,0:T(8,128)(2,1)S(1)}, f16[4,16,512]{2,1,0:T(8,128)(2,1)S(1)}, u32[]{:S(2)}, u32[]{:S(2)}) collective-permute-start(f16[4,16,512]{2,1,0:T(8,128)(2,1)S(1)} %convert_element_type.20), channel_id=1, source_target_pairs={{0,16},{8,24},{16,0},{24,8},{1,17},{9,25},{17,1},{25,9},{2,18},{10... | collective-permute-start | bytes 196616 | tf_op jit(solution)/shard_map/ppermute | solution.py:178
  16.4 4.3 %collective-permute-start.3 = (f16[4,16,512]{2,1,0:T(8,128)(2,1)S(1)}, f16[4,16,512]{2,1,0:T(8,128)(2,1)S(1)}, u32[]{:S(2)}, u32[]{:S(2)}) collective-permute-start(f16[4,16,512]{2,1,0:T(8,128)(2,1)S(1)} %convert_element_type.18), channel_id=1, source_target_pairs={{0,8},{8,0},{16,24},{24,16},{1,9},{9,1},{17,25},{25,17},{2,10},{10... | collective-permute-start | bytes 196616 | tf_op jit(solution)/shard_map/ppermute | solution.py:178

commit v4 on v3

--- a/solution.py
+++ b/solution.py
@@ -9,6 +9,8 @@
 from jax.sharding import PartitionSpec as P
 
 CONTRACT_LAST = (((1,), (1,)), ((), ()))
+SMALLEST = 2.0**-14
+FINER = 2.0**28
 MAX_RETURN = 0.15917969
 MAX_WEIGHT = 0.375
 VMEM = pl.BlockSpec(memory_space=pltpu.VMEM)
@@ -39,7 +41,7 @@
 
 def swap(rows, bit):
     count = lax.axis_size("paths")
-    return lax.ppermute(rows, "paths", [(s, s ^ bit) for s in range(count)])
+    return lax.ppermute(rows, "paths", [(s, s ^ (bit | 1)) for s in range(count)])
 
 
 def stage_kernel(weights_ref, returns_ref, out_ref):
@@ -89,14 +91,11 @@
 
 def encode(part, terms):
     part = part * scale_of(terms)
-    wide = part * 8193.0
-    near = wide - (wide - part)
-    return jnp.where(part < near, -near, near)
+    return jnp.where(part < SMALLEST, part * -FINER, part)
 
 
 def decode(sent, terms):
-    sent = sent.astype(jnp.float32)
-    return (jnp.abs(sent) + (0.75 * 2.0**-12) * sent) * (1 / scale_of(terms))
+    return jnp.where(sent < 0, sent * (-1 / (FINER * scale_of(terms))), sent * (1 / scale_of(terms)))
 
 
 def second_kernel(segments, tile, rows_ref, returns_ref, first_ref, *refs):

time: 21.6 us -> 20.3 us (0.940)
  waiting for transfers between devices: 6.21 us -> 5.56 us
  starting transfers between devices: 10.1 us -> 9.61 us
    ppermute x3, waiting for transfers between devices: 2.17 us -> 1.61 us  [swap(): lax.ppermute(rows, 'paths', [(s, s ^ (bit | 1)) for s in range(count)])]
    ppermute x3, starting transfers between devices: 6.5 us -> 5.99 us  [swap(): lax.ppermute(rows, 'paths', [(s, s ^ (bit | 1)) for s in range(count)])]
  transfers between devices with their start and end apart: 6 -> 6, of which waited for: 6 -> 5; matrix products, arithmetic and copies ran while one was open for 0% -> 0% of each run, Pallas kernels for 7% -> 8%
where the time goes in v4:
time: 20.3 us; the launch traced here: 20.2 us
  starting transfers between devices  9.61 us (47%)
  waiting for transfers between devices  5.56 us (27%)
  Pallas kernels  4.01 us (20%)
  local copies, waits for them, and re-layouts  0.91 us (4%)
    ppermute x3, starting transfers between devices, swap(): lax.ppermute(rows, 'paths', [(s, s ^ (bit | 1)) for s in range(count)])  5.99 us
    pallas_call x6, Pallas kernels, call(): pl.pallas_call(kernel, out_shape=out_shape, in_specs=[HBM if i in kept el...  4.01 us
    ppermute x3, waiting for transfers between devices, shards(): lax.ppermute(parts[k].astype(jnp.float16), 'tm', [(s, s ^ k) for s in ran...  3.95 us
    ppermute x3, starting transfers between devices, shards(): lax.ppermute(parts[k].astype(jnp.float16), 'tm', [(s, s ^ k) for s in ran...  3.62 us
    ppermute x3, waiting for transfers between devices, swap(): lax.ppermute(rows, 'paths', [(s, s ^ (bit | 1)) for s in range(count)])  1.61 us
    unnamed x4, local copies, waits for them, and re-layouts  0.91 us
  transfers between devices with their start and end apart: 6, of which 5 were waited for; matrix products, arithmetic and copies ran while one was open for 0% of the time, Pallas kernels for 8%

profile of v4, /device:TPU:0, one launch (start us, length us, event | category | flops | bytes accessed | tf_op | source)
XLA Modules:
  0.0 20.2 jit_solution(1011275649695440592)
XLA Ops:
  0.0 0.0 copy-start
  0.0 0.5 %collective-permute-start = (bf16[32,64]{1,0:T(8,128)(2,1)}, bf16[32,64]{1,0:T(8,128)(2,1)S(1)}, u32[]{:S(2)}, u32[]{:S(2)}) collective-permute-start(bf16[32,64]{1,0:T(8,128)(2,1)} %weights_ref.1), channel_id=1, source_target_pairs={{0,1},{1,0},{2,3},{3,2},{4,5},{5,4},{6,7},{7,6},{8,9},{9,8},{10,11... | collective-permute-start | bytes 12296 | tf_op jit(solution)/shard_map/ppermute | solution.py:44
  0.5 0.0 copy-start.1
  0.5 0.9 %copy-done.1 = bf16[32,64]{1,0:T(8,128)(2,1)S(1)} copy-done((bf16[32,64]{1,0:T(8,128)(2,1)S(1)}, bf16[32,64]{1,0:T(8,128)(2,1)}, u32[]{:S(2)}) %copy-start.1) | copy-done | bytes 4120
  1.4 0.1 collective-permute-done.other_ref
  1.5 2.7 %collective-permute-start.1 = (bf16[64,64]{1,0:T(8,128)(2,1)S(1)}, bf16[64,64]{1,0:T(8,128)(2,1)S(1)}, u32[]{:S(2)}, u32[]{:S(2)}) collective-permute-start(bf16[64,64]{1,0:T(8,128)(2,1)S(1)} %merge1.1.rows_ref), channel_id=1, source_target_pairs={{0,3},{1,2},{2,1},{3,0},{4,7},{5,6},{6,5},{7,4},{8,11},{9,10},{10,... | collective-permute-start | bytes 24584 | tf_op jit(solution)/shard_map/ppermute | solution.py:44
  4.2 1.4 %collective-permute-done.1.other_ref = bf16[64,64]{1,0:T(8,128)(2,1)S(1)} collective-permute-done((bf16[64,64]{1,0:T(8,128)(2,1)S(1)}, bf16[64,64]{1,0:T(8,128)(2,1)S(1)}, u32[]{:S(2)}, u32[]{:S(2)}) %collective-permute-start.1) | collective-permute-done | bytes 8224 | tf_op jit(solution)/shard_map/ppermute | solution.py:44
  5.7 2.8 %collective-permute-start.2 = (bf16[128,64]{1,0:T(8,128)(2,1)S(1)}, bf16[128,64]{1,0:T(8,128)(2,1)S(1)}, u32[]{:S(2)}, u32[]{:S(2)}) collective-permute-start(bf16[128,64]{1,0:T(8,128)(2,1)S(1)} %merge2.1.rows_ref), channel_id=1, source_target_pairs={{0,5},{1,4},{2,7},{3,6},{4,1},{5,0},{6,3},{7,2},{8,13},{9,12},{10,... | collective-permute-start | bytes 49160 | tf_op jit(solution)/shard_map/ppermute | solution.py:44
  8.5 0.0 copy-done
  8.5 1.6 %first.1.first_ref = f32[32,128,256]{2,1,0:T(8,128)S(1)} custom-call(bf16[128,64]{1,0:T(8,128)(2,1)S(1)} %merge2.1.rows_ref, bf16[32,512,256]{2,1,0:T(8,128)(2,1)S(1)} %copy-done), custom_call_target="tpu_custom_call" | custom-call | flops 536870912 | bytes 4194304 | tf_op jit(solution)/shard_map/first/pallas_call | solution.py:30
  10.1 0.0 collective-permute-done.2.rows_ref
  10.1 1.7 %second.1 = (f32[4,16,512]{2,1,0:T(8,128)S(1)}, f32[4,16,512]{2,1,0:T(8,128)S(1)}, f32[4,16,512]{2,1,0:T(8,128)S(1)}, f32[4,16,512]{2,1,0:T(8,128)S(1)}) custom-call(bf16[128,64]{1,0:T(8,128)(2,1)S(1)} %collective-permute-done.2.rows_ref, bf16[32,512,256]{2,1,0:T(8,128)(2,1)S(1)} %copy-done, f32[32,128,256]{2,1,0:T(8,128)S(1)} %first.1.first_ref), custom_call_target="tpu_custom_call" | custom-call | flops 536870912 | bytes 4194304 | tf_op jit(solution)/shard_map/second/pallas_call | solution.py:30
  11.9 2.8 %collective-permute-start.5 = (f16[4,16,512]{2,1,0:T(8,128)(2,1)S(1)}, f16[4,16,512]{2,1,0:T(8,128)(2,1)S(1)}, u32[]{:S(2)}, u32[]{:S(2)}) collective-permute-start(f16[4,16,512]{2,1,0:T(8,128)(2,1)S(1)} %convert_element_type.22), channel_id=1, source_target_pairs={{0,24},{8,16},{16,8},{24,0},{1,25},{9,17},{17,9},{25,1},{2,26},{10... | collective-permute-start | bytes 196616 | tf_op jit(solution)/shard_map/ppermute | solution.py:177
  14.6 0.5 %collective-permute-start.4 = (f16[4,16,512]{2,1,0:T(8,128)(2,1)S(1)}, f16[4,16,512]{2,1,0:T(8,128)(2,1)S(1)}, u32[]{:S(2)}, u32[]{:S(2)}) collective-permute-start(f16[4,16,512]{2,1,0:T(8,128)(2,1)S(1)} %convert_element_type.20), channel_id=1, source_target_pairs={{0,16},{8,24},{16,0},{24,8},{1,17},{9,25},{17,1},{25,9},{2,18},{10... | collective-permute-start | bytes 196616 | tf_op jit(solution)/shard_map/ppermute | solution.py:177
  15.2 0.3 %collective-permute-start.3 = (f16[4,16,512]{2,1,0:T(8,128)(2,1)S(1)}, f16[4,16,512]{2,1,0:T(8,128)(2,1)S(1)}, u32[]{:S(2)}, u32[]{:S(2)}) collective-permute-start(f16[4,16,512]{2,1,0:T(8,128)(2,1)S(1)} %convert_element_type.18), channel_id=1, source_target_pairs={{0,8},{8,0},{16,24},{24,16},{1,9},{9,1},{17,25},{25,17},{2,10},{10... | collective-permute-start | bytes 196616 | tf_op jit(solution)/shard_map/ppermute | solution.py:177
  15.5 1.6 %collective-permute-done.5 = f16[4,16,512]{2,1,0:T(8,128)(2,1)S(1)} collective-permute-done((f16[4,16,512]{2,1,0:T(8,128)(2,1)S(1)}, f16[4,16,512]{2,1,0:T(8,128)(2,1)S(1)}, u32[]{:S(2)}, u32[]{:S(2)}) %collective-permute-start.5) | collective-permute-done | bytes 65568 | tf_op jit(solution)/shard_map/ppermute | solution.py:177
  17.2 1.7 %collective-permute-done.4 = f16[4,16,512]{2,1,0:T(8,128)(2,1)S(1)} collective-permute-done((f16[4,16,512]{2,1,0:T(8,128)(2,1)S(1)}, f16[4,16,512]{2,1,0:T(8,128)(2,1)S(1)}, u32[]{:S(2)}, u32[]{:S(2)}) %collective-permute-start.4) | collective-permute-done | bytes 65568 | tf_op jit(solution)/shard_map/ppermute | solution.py:177
  18.9 0.6 %collective-permute-done.3 = f16[4,16,512]{2,1,0:T(8,128)(2,1)S(1)} collective-permute-done((f16[4,16,512]{2,1,0:T(8,128)(2,1)S(1)}, f16[4,16,512]{2,1,0:T(8,128)(2,1)S(1)}, u32[]{:S(2)}, u32[]{:S(2)}) %collective-permute-start.3) | collective-permute-done | bytes 65568 | tf_op jit(solution)/shard_map/ppermute | solution.py:177
  19.5 0.7 %join.1 = f32[16,512]{1,0:T(8,128)} custom-call(f32[4,16,512]{2,1,0:T(8,128)S(1)} %get-tuple-element.9.refs_0_, f32[4,16,512]{2,1,0:T(8,128)S(1)} %convert_element_type.19.refs_1_, f32[4,16,512]{2,1,0:T(8,128)S(1)} %convert_element_type.21.refs_2_, f32[4,16,512]{2,1,0:T(8,128)S(1)} %convert_element_type.23.refs_3_), custom_call_target="tpu_custom_call" | custom-call | bytes 262144 | tf_op jit(solution)/shard_map/join/pallas_call | solution.py:30
  (9 shorter events, 0.1 us)
Async XLA Ops:
  0.0 8.5 %copy-start = (bf16[32,512,256]{2,1,0:T(8,128)(2,1)S(1)}, bf16[32,512,256]{2,1,0:T(8,128)(2,1)}, u32[]{:S(2)}) copy-start(bf16[32,512,256]{2,1,0:T(8,128)(2,1)} %returns_ref.5) | copy-start | bytes 25165828
  0.0 1.5 %collective-permute-start = (bf16[32,64]{1,0:T(8,128)(2,1)}, bf16[32,64]{1,0:T(8,128)(2,1)S(1)}, u32[]{:S(2)}, u32[]{:S(2)}) collective-permute-start(bf16[32,64]{1,0:T(8,128)(2,1)} %weights_ref.1), channel_id=1, source_target_pairs={{0,1},{1,0},{2,3},{3,2},{4,5},{5,4},{6,7},{7,6},{8,9},{9,8},{10,11... | collective-permute-start | bytes 12296 | tf_op jit(solution)/shard_map/ppermute | solution.py:44
  0.5 0.9 %copy-start.1 = (bf16[32,64]{1,0:T(8,128)(2,1)S(1)}, bf16[32,64]{1,0:T(8,128)(2,1)}, u32[]{:S(2)}) copy-start(bf16[32,64]{1,0:T(8,128)(2,1)} %weights_ref.1) | copy-start | bytes 12292
  1.5 4.1 %collective-permute-start.1 = (bf16[64,64]{1,0:T(8,128)(2,1)S(1)}, bf16[64,64]{1,0:T(8,128)(2,1)S(1)}, u32[]{:S(2)}, u32[]{:S(2)}) collective-permute-start(bf16[64,64]{1,0:T(8,128)(2,1)S(1)} %merge1.1.rows_ref), channel_id=1, source_target_pairs={{0,3},{1,2},{2,1},{3,0},{4,7},{5,6},{6,5},{7,4},{8,11},{9,10},{10,... | collective-permute-start | bytes 24584 | tf_op jit(solution)/shard_map/ppermute | solution.py:44
  5.7 4.4 %collective-permute-start.2 = (bf16[128,64]{1,0:T(8,128)(2,1)S(1)}, bf16[128,64]{1,0:T(8,128)(2,1)S(1)}, u32[]{:S(2)}, u32[]{:S(2)}) collective-permute-start(bf16[128,64]{1,0:T(8,128)(2,1)S(1)} %merge2.1.rows_ref), channel_id=1, source_target_pairs={{0,5},{1,4},{2,7},{3,6},{4,1},{5,0},{6,3},{7,2},{8,13},{9,12},{10,... | collective-permute-start | bytes 49160 | tf_op jit(solution)/shard_map/ppermute | solution.py:44
  11.9 5.3 %collective-permute-start.5 = (f16[4,16,512]{2,1,0:T(8,128)(2,1)S(1)}, f16[4,16,512]{2,1,0:T(8,128)(2,1)S(1)}, u32[]{:S(2)}, u32[]{:S(2)}) collective-permute-start(f16[4,16,512]{2,1,0:T(8,128)(2,1)S(1)} %convert_element_type.22), channel_id=1, source_target_pairs={{0,24},{8,16},{16,8},{24,0},{1,25},{9,17},{17,9},{25,1},{2,26},{10... | collective-permute-start | bytes 196616 | tf_op jit(solution)/shard_map/ppermute | solution.py:177
  14.6 4.3 %collective-permute-start.4 = (f16[4,16,512]{2,1,0:T(8,128)(2,1)S(1)}, f16[4,16,512]{2,1,0:T(8,128)(2,1)S(1)}, u32[]{:S(2)}, u32[]{:S(2)}) collective-permute-start(f16[4,16,512]{2,1,0:T(8,128)(2,1)S(1)} %convert_element_type.20), channel_id=1, source_target_pairs={{0,16},{8,24},{16,0},{24,8},{1,17},{9,25},{17,1},{25,9},{2,18},{10... | collective-permute-start | bytes 196616 | tf_op jit(solution)/shard_map/ppermute | solution.py:177
  15.2 4.3 %collective-permute-start.3 = (f16[4,16,512]{2,1,0:T(8,128)(2,1)S(1)}, f16[4,16,512]{2,1,0:T(8,128)(2,1)S(1)}, u32[]{:S(2)}, u32[]{:S(2)}) collective-permute-start(f16[4,16,512]{2,1,0:T(8,128)(2,1)S(1)} %convert_element_type.18), channel_id=1, source_target_pairs={{0,8},{8,0},{16,24},{24,16},{1,9},{9,1},{17,25},{25,17},{2,10},{10... | collective-permute-start | bytes 196616 | tf_op jit(solution)/shard_map/ppermute | solution.py:177

commit v5 on v4

v5 whole, which is shorter than its diff:
```python
import functools
import math

import jax
import jax.numpy as jnp
from jax import lax
from jax.experimental import pallas as pl
from jax.experimental.pallas import tpu as pltpu
from jax.sharding import PartitionSpec as P

SMALLEST = 2.0**-14
FINER = 2.0**28
MAX_RETURN = 0.15917969
MAX_WEIGHT = 0.375
VMEM = pl.BlockSpec(memory_space=pltpu.VMEM)
HBM = pl.BlockSpec(memory_space=pltpu.HBM)


def call(kernel, name, out_shape, args, scratch=(), kept=(), limit=8, flops=0, moved=0):
    args = [
        pltpu.with_memory_space_constraint(a, pltpu.HBM) if i in kept else a
        for i, a in enumerate(args)
    ]
    several = isinstance(out_shape, (list, tuple))
    return pl.pallas_call(
        kernel,
        out_shape=out_shape,
        in_specs=[HBM if i in kept else VMEM for i in range(len(args))],
        out_specs=[VMEM] * len(out_shape) if several else VMEM,
        scratch_shapes=list(scratch),
        compiler_params=pltpu.CompilerParams(vmem_limit_bytes=limit * 2**20),
        cost_estimate=pl.CostEstimate(flops=flops, bytes_accessed=moved, transcendentals=0),
        name=name,
    )(*args)


def swap(rows, bit):
    count = lax.axis_size("paths")
    return lax.ppermute(rows, "paths", [(s, s ^ (bit | 1)) for s in range(count)])


def stage_kernel(weights_ref, returns_ref, out_ref):
    out_ref[...] = weights_ref[...]


def pair_kernel(rows_ref, other_ref, out_ref):
    ports = rows_ref.shape[1]
    first = lax.axis_index("paths") % 2 == 0
    mine, other = rows_ref[...], other_ref[...]
    out_ref[:, :ports] = jnp.where(first, mine, other)
    out_ref[:, ports:] = jnp.where(first, other, mine)


def merge_kernel(bit, rows_ref, other_ref, out_ref):
    count = rows_ref.shape[0]
    upper = (lax.axis_index("paths") // bit) % 2
    out_ref[pl.ds(pl.multiple_of(upper * count, count), count)] = rows_ref[...]
    out_ref[pl.ds(pl.multiple_of((1 - upper) * count, count), count)] = other_ref[...]


def lay_out(shard, rows_ref, both_ref):
    ports = rows_ref.shape[1] // 2
    assets = both_ref.shape[0] // 2
    both_ref[...] = jnp.zeros_like(both_ref)
    for h in range(2):
        for n in range(assets // shard):
            block = slice(n // 2 * shard, (n // 2 + 1) * shard)
            core = slice(n % 2 * ports, (n % 2 + 1) * ports)
            at = h * assets + n * shard
            both_ref[at : at + shard, h * ports : (h + 1) * ports] = rows_ref[block, core]


def half_profit(both, returns_ref, t, half, start, count):
    paths, assets = returns_ref.shape[1:]
    columns = pl.ds(pl.multiple_of(half * (assets // 2), assets // 2), assets // 2)
    rows = [returns_ref[t, pl.ds(h * (paths // 2) + start, count), columns] for h in range(2)]
    return jnp.dot(jnp.concatenate(rows, axis=1), both, preferred_element_type=jnp.float32)


def first_kernel(shard, rows_ref, returns_ref, out_ref, both_ref):
    half = lax.axis_index("paths") // (lax.axis_size("paths") // 2)
    lay_out(shard, rows_ref, both_ref)
    both = both_ref[...]
    for t in range(returns_ref.shape[0]):
        out_ref[t] = half_profit(both, returns_ref, t, half, 0, out_ref.shape[1])


def scale_of(terms):
    return 2.0 ** math.floor(math.log2(65504 / (terms * MAX_RETURN * MAX_WEIGHT)))


def encode(part, terms):
    part = part * scale_of(terms)
    return jnp.where(part < SMALLEST, part * -FINER, part)


def decode(sent, terms):
    return jnp.where(sent < 0, sent * (-1 / (FINER * scale_of(terms))), sent * (1 / scale_of(terms)))


def second_kernel(segments, shard, tile, rows_ref, returns_ref, first_ref, *refs):
    out_ref, both_ref, stats = refs
    steps, paths, assets = returns_ref.shape
    ports = rows_ref.shape[1] // 2
    width = ports // segments
    half = 1 - lax.axis_index("paths") // (lax.axis_size("paths") // 2)
    lay_out(shard, rows_ref, both_ref)
    both = both_ref[...]
    stats[...] = jnp.zeros_like(stats)
    own = lax.axis_index("tm")
    block = min(128, paths // 2)
    for start in range(0, paths // 2, block):
        for g in range(0, steps, tile):
            profits = [
                half_profit(both, returns_ref, g + i, half, start, block) for i in range(tile)
            ]
            for q in range(0, block, 16):
                at = slice(start + q, start + q + 16)
                value, peak, low, fall = (stats[n, at] for n in range(4))
                for i in range(tile):
                    value = value + (first_ref[g + i, at] + profits[i][q : q + 16])
                    peak = jnp.maximum(peak, value)
                    low = jnp.minimum(low, value)
                    fall = jnp.maximum(fall, peak - value)
                for n, new in enumerate((value, peak, low, fall)):
                    stats[n, at] = new
        value, peak, low, fall = (stats[n, start : start + block] for n in range(4))
        for n, part in enumerate((fall, -low, peak - value, value - low)):
            turned = part.T
            for h in range(2):
                put = slice(h * (paths // 2) + start, h * (paths // 2) + start + block)
                for s in range(segments):
                    at = h * ports + s * width
                    exact = turned[at : at + width]
                    coded = encode(exact, steps * assets)
                    out_ref[own ^ s, n, :, put] = jnp.where(own == s, exact, coded)


def join_kernel(segments, terms, *refs):
    ins, out_ref, ordered = refs[:segments], refs[segments], refs[segments + 1]
    own = lax.axis_index("tm")
    for k in range(segments):
        ordered[own ^ k] = ins[0][0] if k == 0 else decode(ins[k][...], terms)
    fall = ordered[0, 0]
    drop = ordered[0, 2]
    for s in range(1, segments):
        below = ordered[s, 1]
        fall = jnp.maximum(jnp.maximum(fall, ordered[s, 0]), drop + below)
        drop = jnp.maximum(drop + below - ordered[s, 3], ordered[s, 2])
    out_ref[...] = fall


def shards(returns, weights):
    segments = lax.axis_size("tm")
    count = lax.axis_size("paths")
    steps, paths, assets = returns.shape
    shard, ports = weights.shape
    width = ports // segments
    held = jax.ShapeDtypeStruct((steps, paths // 2, 2 * ports), jnp.float32)
    both = pltpu.VMEM((assets, 2 * ports), weights.dtype)
    work = 2 * steps * paths * assets * ports

    rows = call(
        stage_kernel, "stage", jax.ShapeDtypeStruct(weights.shape, weights.dtype),
        [weights, returns], kept=(1,), flops=work, moved=returns.size * 2,
    )
    rows = call(
        pair_kernel, "pair", jax.ShapeDtypeStruct((shard, 2 * ports), rows.dtype),
        [rows, swap(weights, 1)],
    )
    bit = 2
    while 2 * bit < count:
        rows = call(
            functools.partial(merge_kernel, bit), f"merge{bit}",
            jax.ShapeDtypeStruct((2 * rows.shape[0], 2 * ports), rows.dtype),
            [rows, swap(rows, bit)],
        )
        bit *= 2
    other = swap(rows, bit)
    first = call(
        functools.partial(first_kernel, shard), "first", held, [rows, returns], scratch=[both],
        flops=work, moved=returns.size,
    )
    parts = call(
        functools.partial(second_kernel, segments, shard, min(steps, 8)), "second",
        jax.ShapeDtypeStruct((segments, 4, width, paths), jnp.float32), [other, returns, first],
        scratch=[both, pltpu.VMEM((4, paths // 2, 2 * ports), jnp.float32)],
        flops=work, moved=returns.size,
    )
    arrived = {
        k: lax.ppermute(
            parts[k].astype(jnp.float16), "tm", [(s, s ^ k) for s in range(segments)]
        ).astype(jnp.float32)
        for k in range(1, segments)
    }
    return call(
        functools.partial(join_kernel, segments, steps * assets), "join",
        jax.ShapeDtypeStruct((width, paths), jnp.float32),
        [parts] + [arrived[k] for k in range(1, segments)],
        scratch=[pltpu.VMEM((segments, 4, width, paths), jnp.float32)],
        moved=4 * parts.size,
    )


def solution(mesh):
    in_specs = (P("tm", "paths", None), P("paths", None))
    out_specs = P("tm", "paths")
    return jax.shard_map(shards, mesh=mesh, in_specs=in_specs, out_specs=out_specs, check_vma=False)
```

time: 20.3 us -> 19.9 us (0.980)
  Pallas kernels: 4.01 us -> 3.63 us
    pallas_call x6, Pallas kernels: 4.01 us -> 3.63 us  [call(): pl.pallas_call(kernel, out_shape=out_shape, in_specs=[HBM if i in kept el...]
  transfers between devices with their start and end apart: 6 -> 6, of which waited for: 5 -> 6; matrix products, arithmetic and copies ran while one was open for 0% -> 0% of each run, Pallas kernels for 8% -> 7%
where the time goes in v5:
time: 19.9 us; the launch traced here: 19.7 us
  starting transfers between devices  9.44 us (47%)
  waiting for transfers between devices  5.57 us (28%)
  Pallas kernels  3.63 us (18%)
  local copies, waits for them, and re-layouts  0.94 us (5%)
    ppermute x3, starting transfers between devices, swap(): lax.ppermute(rows, 'paths', [(s, s ^ (bit | 1)) for s in range(count)])  5.89 us
    ppermute x3, waiting for transfers between devices, shards(): lax.ppermute(parts[k].astype(jnp.float16), 'tm', [(s, s ^ k) for s in ran...  3.95 us
    pallas_call x6, Pallas kernels, call(): pl.pallas_call(kernel, out_shape=out_shape, in_specs=[HBM if i in kept el...  3.63 us
    ppermute x3, starting transfers between devices, shards(): lax.ppermute(parts[k].astype(jnp.float16), 'tm', [(s, s ^ k) for s in ran...  3.55 us
    ppermute x3, waiting for transfers between devices, swap(): lax.ppermute(rows, 'paths', [(s, s ^ (bit | 1)) for s in range(count)])  1.62 us
    unnamed x4, local copies, waits for them, and re-layouts  0.91 us
  transfers between devices with their start and end apart: 6, of which 6 were waited for; matrix products, arithmetic and copies ran while one was open for 0% of the time, Pallas kernels for 7%

profile of v5, /device:TPU:0, one launch (start us, length us, event | category | flops | bytes accessed | tf_op | source)
XLA Modules:
  0.0 19.7 jit_solution(18321425731025887613)
XLA Ops:
  0.0 0.0 copy-start
  0.0 0.5 %collective-permute-start = (bf16[32,64]{1,0:T(8,128)(2,1)}, bf16[32,64]{1,0:T(8,128)(2,1)S(1)}, u32[]{:S(2)}, u32[]{:S(2)}) collective-permute-start(bf16[32,64]{1,0:T(8,128)(2,1)} %weights_ref.1), channel_id=1, source_target_pairs={{0,1},{1,0},{2,3},{3,2},{4,5},{5,4},{6,7},{7,6},{8,9},{9,8},{10,11... | collective-permute-start | bytes 12296 | tf_op jit(solution)/shard_map/ppermute | solution.py:39
  0.5 0.0 copy-start.1
  0.5 0.9 %copy-done.1 = bf16[32,64]{1,0:T(8,128)(2,1)S(1)} copy-done((bf16[32,64]{1,0:T(8,128)(2,1)S(1)}, bf16[32,64]{1,0:T(8,128)(2,1)}, u32[]{:S(2)}) %copy-start.1) | copy-done | bytes 4120
  1.4 0.1 collective-permute-done.other_ref
  1.5 0.1 pair.1.rows_ref
  1.6 2.7 %collective-permute-start.1 = (bf16[32,128]{1,0:T(8,128)(2,1)S(1)}, bf16[32,128]{1,0:T(8,128)(2,1)S(1)}, u32[]{:S(2)}, u32[]{:S(2)}) collective-permute-start(bf16[32,128]{1,0:T(8,128)(2,1)S(1)} %pair.1.rows_ref), channel_id=1, source_target_pairs={{0,3},{1,2},{2,1},{3,0},{4,7},{5,6},{6,5},{7,4},{8,11},{9,10},{10,... | collective-permute-start | bytes 24584 | tf_op jit(solution)/shard_map/ppermute | solution.py:39
  4.3 1.4 %collective-permute-done.1.other_ref = bf16[32,128]{1,0:T(8,128)(2,1)S(1)} collective-permute-done((bf16[32,128]{1,0:T(8,128)(2,1)S(1)}, bf16[32,128]{1,0:T(8,128)(2,1)S(1)}, u32[]{:S(2)}, u32[]{:S(2)}) %collective-permute-start.1) | collective-permute-done | bytes 8224 | tf_op jit(solution)/shard_map/ppermute | solution.py:39
  5.7 2.7 %collective-permute-start.2 = (bf16[64,128]{1,0:T(8,128)(2,1)S(1)}, bf16[64,128]{1,0:T(8,128)(2,1)S(1)}, u32[]{:S(2)}, u32[]{:S(2)}) collective-permute-start(bf16[64,128]{1,0:T(8,128)(2,1)S(1)} %merge2.1.rows_ref), channel_id=1, source_target_pairs={{0,5},{1,4},{2,7},{3,6},{4,1},{5,0},{6,3},{7,2},{8,13},{9,12},{10,... | collective-permute-start | bytes 49160 | tf_op jit(solution)/shard_map/ppermute | solution.py:39
  8.4 0.0 copy-done
  8.4 1.3 %first.1.first_ref = f32[32,256,128]{2,1,0:T(8,128)S(1)} custom-call(bf16[64,128]{1,0:T(8,128)(2,1)S(1)} %merge2.1.rows_ref, bf16[32,512,256]{2,1,0:T(8,128)(2,1)S(1)} %copy-done), custom_call_target="tpu_custom_call" | custom-call | flops 536870912 | bytes 4194304 | tf_op jit(solution)/shard_map/first/pallas_call | solution.py:25
  9.7 0.1 collective-permute-done.2.rows_ref
  9.8 1.5 %second.1.refs_0_ = f32[4,4,16,512]{3,2,1,0:T(8,128)S(1)} custom-call(bf16[64,128]{1,0:T(8,128)(2,1)S(1)} %collective-permute-done.2.rows_ref, bf16[32,512,256]{2,1,0:T(8,128)(2,1)S(1)} %copy-done, f32[32,256,128]{2,1,0:T(8,128)S(1)} %first.1.first_ref), custom_call_target="tpu_custom_call" | custom-call | flops 536870912 | bytes 4194304 | tf_op jit(solution)/shard_map/second/pallas_call | solution.py:25
  11.5 2.8 %collective-permute-start.5 = (f16[4,16,512]{2,1,0:T(8,128)(2,1)S(1)}, f16[4,16,512]{2,1,0:T(8,128)(2,1)S(1)}, u32[]{:S(2)}, u32[]{:S(2)}) collective-permute-start(f16[4,16,512]{2,1,0:T(8,128)(2,1)S(1)} %get-tuple-element.5), channel_id=1, source_target_pairs={{0,24},{8,16},{16,8},{24,0},{1,25},{9,17},{17,9},{25,1},{2,26},{10... | collective-permute-start | bytes 196616 | tf_op jit(solution)/shard_map/ppermute | solution.py:191
  14.2 0.5 %collective-permute-start.4 = (f16[4,16,512]{2,1,0:T(8,128)(2,1)S(1)}, f16[4,16,512]{2,1,0:T(8,128)(2,1)S(1)}, u32[]{:S(2)}, u32[]{:S(2)}) collective-permute-start(f16[4,16,512]{2,1,0:T(8,128)(2,1)S(1)} %get-tuple-element.6), channel_id=1, source_target_pairs={{0,16},{8,24},{16,0},{24,8},{1,17},{9,25},{17,1},{25,9},{2,18},{10... | collective-permute-start | bytes 196616 | tf_op jit(solution)/shard_map/ppermute | solution.py:191
  14.7 0.3 %collective-permute-start.3 = (f16[4,16,512]{2,1,0:T(8,128)(2,1)S(1)}, f16[4,16,512]{2,1,0:T(8,128)(2,1)S(1)}, u32[]{:S(2)}, u32[]{:S(2)}) collective-permute-start(f16[4,16,512]{2,1,0:T(8,128)(2,1)S(1)} %get-tuple-element.7), channel_id=1, source_target_pairs={{0,8},{8,0},{16,24},{24,16},{1,9},{9,1},{17,25},{25,17},{2,10},{10... | collective-permute-start | bytes 196616 | tf_op jit(solution)/shard_map/ppermute | solution.py:191
  15.0 1.7 %collective-permute-done.5 = f16[4,16,512]{2,1,0:T(8,128)(2,1)S(1)} collective-permute-done((f16[4,16,512]{2,1,0:T(8,128)(2,1)S(1)}, f16[4,16,512]{2,1,0:T(8,128)(2,1)S(1)}, u32[]{:S(2)}, u32[]{:S(2)}) %collective-permute-start.5) | collective-permute-done | bytes 65568 | tf_op jit(solution)/shard_map/ppermute | solution.py:191
  16.7 1.7 %collective-permute-done.4 = f16[4,16,512]{2,1,0:T(8,128)(2,1)S(1)} collective-permute-done((f16[4,16,512]{2,1,0:T(8,128)(2,1)S(1)}, f16[4,16,512]{2,1,0:T(8,128)(2,1)S(1)}, u32[]{:S(2)}, u32[]{:S(2)}) %collective-permute-start.4) | collective-permute-done | bytes 65568 | tf_op jit(solution)/shard_map/ppermute | solution.py:191
  18.5 0.5 %collective-permute-done.3 = f16[4,16,512]{2,1,0:T(8,128)(2,1)S(1)} collective-permute-done((f16[4,16,512]{2,1,0:T(8,128)(2,1)S(1)}, f16[4,16,512]{2,1,0:T(8,128)(2,1)S(1)}, u32[]{:S(2)}, u32[]{:S(2)}) %collective-permute-start.3) | collective-permute-done | bytes 65568 | tf_op jit(solution)/shard_map/ppermute | solution.py:191
  19.0 0.7 %join.1 = f32[16,512]{1,0:T(8,128)} custom-call(f32[4,4,16,512]{3,2,1,0:T(8,128)S(1)} %second.1.refs_0_, f32[4,16,512]{2,1,0:T(8,128)S(1)} %convert_element_type.22.refs_1_, f32[4,16,512]{2,1,0:T(8,128)S(1)} %convert_element_type.24.refs_2_, f32[4,16,512]{2,1,0:T(8,128)S(1)} %convert_element_type.26.refs_3_), custom_call_target="tpu_custom_call" | custom-call | bytes 524288 | tf_op jit(solution)/shard_map/join/pallas_call | solution.py:25
  (7 shorter events, 0.1 us)
Async XLA Ops:
  0.0 8.4 %copy-start = (bf16[32,512,256]{2,1,0:T(8,128)(2,1)S(1)}, bf16[32,512,256]{2,1,0:T(8,128)(2,1)}, u32[]{:S(2)}) copy-start(bf16[32,512,256]{2,1,0:T(8,128)(2,1)} %returns_ref.5) | copy-start | bytes 25165828
  0.0 1.5 %collective-permute-start = (bf16[32,64]{1,0:T(8,128)(2,1)}, bf16[32,64]{1,0:T(8,128)(2,1)S(1)}, u32[]{:S(2)}, u32[]{:S(2)}) collective-permute-start(bf16[32,64]{1,0:T(8,128)(2,1)} %weights_ref.1), channel_id=1, source_target_pairs={{0,1},{1,0},{2,3},{3,2},{4,5},{5,4},{6,7},{7,6},{8,9},{9,8},{10,11... | collective-permute-start | bytes 12296 | tf_op jit(solution)/shard_map/ppermute | solution.py:39
  0.5 0.9 %copy-start.1 = (bf16[32,64]{1,0:T(8,128)(2,1)S(1)}, bf16[32,64]{1,0:T(8,128)(2,1)}, u32[]{:S(2)}) copy-start(bf16[32,64]{1,0:T(8,128)(2,1)} %weights_ref.1) | copy-start | bytes 12292
  1.6 4.0 %collective-permute-start.1 = (bf16[32,128]{1,0:T(8,128)(2,1)S(1)}, bf16[32,128]{1,0:T(8,128)(2,1)S(1)}, u32[]{:S(2)}, u32[]{:S(2)}) collective-permute-start(bf16[32,128]{1,0:T(8,128)(2,1)S(1)} %pair.1.rows_ref), channel_id=1, source_target_pairs={{0,3},{1,2},{2,1},{3,0},{4,7},{5,6},{6,5},{7,4},{8,11},{9,10},{10,... | collective-permute-start | bytes 24584 | tf_op jit(solution)/shard_map/ppermute | solution.py:39
  5.7 4.2 %collective-permute-start.2 = (bf16[64,128]{1,0:T(8,128)(2,1)S(1)}, bf16[64,128]{1,0:T(8,128)(2,1)S(1)}, u32[]{:S(2)}, u32[]{:S(2)}) collective-permute-start(bf16[64,128]{1,0:T(8,128)(2,1)S(1)} %merge2.1.rows_ref), channel_id=1, source_target_pairs={{0,5},{1,4},{2,7},{3,6},{4,1},{5,0},{6,3},{7,2},{8,13},{9,12},{10,... | collective-permute-start | bytes 49160 | tf_op jit(solution)/shard_map/ppermute | solution.py:39
  11.5 5.3 %collective-permute-start.5 = (f16[4,16,512]{2,1,0:T(8,128)(2,1)S(1)}, f16[4,16,512]{2,1,0:T(8,128)(2,1)S(1)}, u32[]{:S(2)}, u32[]{:S(2)}) collective-permute-start(f16[4,16,512]{2,1,0:T(8,128)(2,1)S(1)} %get-tuple-element.5), channel_id=1, source_target_pairs={{0,24},{8,16},{16,8},{24,0},{1,25},{9,17},{17,9},{25,1},{2,26},{10... | collective-permute-start | bytes 196616 | tf_op jit(solution)/shard_map/ppermute | solution.py:191
  14.2 4.3 %collective-permute-start.4 = (f16[4,16,512]{2,1,0:T(8,128)(2,1)S(1)}, f16[4,16,512]{2,1,0:T(8,128)(2,1)S(1)}, u32[]{:S(2)}, u32[]{:S(2)}) collective-permute-start(f16[4,16,512]{2,1,0:T(8,128)(2,1)S(1)} %get-tuple-element.6), channel_id=1, source_target_pairs={{0,16},{8,24},{16,0},{24,8},{1,17},{9,25},{17,1},{25,9},{2,18},{10... | collective-permute-start | bytes 196616 | tf_op jit(solution)/shard_map/ppermute | solution.py:191
  14.7 4.3 %collective-permute-start.3 = (f16[4,16,512]{2,1,0:T(8,128)(2,1)S(1)}, f16[4,16,512]{2,1,0:T(8,128)(2,1)S(1)}, u32[]{:S(2)}, u32[]{:S(2)}) collective-permute-start(f16[4,16,512]{2,1,0:T(8,128)(2,1)S(1)} %get-tuple-element.7), channel_id=1, source_target_pairs={{0,8},{8,0},{16,24},{24,16},{1,9},{9,1},{17,25},{25,17},{2,10},{10... | collective-permute-start | bytes 196616 | tf_op jit(solution)/shard_map/ppermute | solution.py:191

commit v6 on v5

--- a/solution.py
+++ b/solution.py
@@ -136,18 +136,44 @@
                     out_ref[own ^ s, n, :, put] = jnp.where(own == s, exact, coded)
 
 
-def join_kernel(segments, terms, *refs):
-    ins, out_ref, ordered = refs[:segments], refs[segments], refs[segments + 1]
+def join_two(a, b):
+    end = a[3] - a[1]
+    below = jnp.maximum(a[1], b[1] - end)
+    return (
+        jnp.maximum(jnp.maximum(a[0], b[0]), a[2] + b[1]),
+        below,
+        jnp.maximum(a[2] + b[1] - b[3], b[2]),
+        end + (b[3] - b[1]) + below,
+    )
+
+
+def join_tree(nodes, bit):
     own = lax.axis_index("tm")
-    for k in range(segments):
-        ordered[own ^ k] = ins[0][0] if k == 0 else decode(ins[k][...], terms)
-    fall = ordered[0, 0]
-    drop = ordered[0, 2]
-    for s in range(1, segments):
-        below = ordered[s, 1]
-        fall = jnp.maximum(jnp.maximum(fall, ordered[s, 0]), drop + below)
-        drop = jnp.maximum(drop + below - ordered[s, 3], ordered[s, 2])
-    out_ref[...] = fall
+    while len(nodes) > 1:
+        later = (own // bit) % 2 == 1
+        nodes = [
+            join_two(
+                [jnp.where(later, y, x) for x, y in zip(a, b)],
+                [jnp.where(later, x, y) for x, y in zip(a, b)],
+            )
+            for a, b in zip(nodes[::2], nodes[1::2])
+        ]
+        bit *= 2
+    return nodes[0]
+
+
+def far_kernel(terms, *refs):
+    nodes = [[decode(ref[n], terms) for n in range(4)] for ref in refs[:-1]]
+    for n, part in enumerate(join_tree(nodes, 1)):
+        refs[-1][n] = part
+
+
+def join_kernel(terms, own_ref, *refs):
+    near, (far_ref, out_ref) = refs[:-2], refs[-2:]
+    nodes = [[own_ref[0, n] for n in range(4)]]
+    nodes += [[decode(ref[n], terms) for n in range(4)] for ref in near]
+    far = [far_ref[n] for n in range(4)]
+    out_ref[...] = join_tree([join_tree(nodes, 1), far], len(nodes))[0]
 
 
 def shards(returns, weights):
@@ -182,7 +208,7 @@
         flops=work, moved=returns.size,
     )
     parts = call(
-        functools.partial(second_kernel, segments, shard, min(steps, 8)), "second",
+        functools.partial(second_kernel, segments, shard, min(steps, 32)), "second",
         jax.ShapeDtypeStruct((segments, 4, width, paths), jnp.float32), [other, returns, first],
         scratch=[both, pltpu.VMEM((4, paths // 2, 2 * ports), jnp.float32)],
         flops=work, moved=returns.size,
@@ -193,12 +219,15 @@
         ).astype(jnp.float32)
         for k in range(1, segments)
     }
+    far = call(
+        functools.partial(far_kernel, steps * assets), "far",
+        jax.ShapeDtypeStruct((4, width, paths), jnp.float32),
+        [arrived[k] for k in range(segments // 2, segments)], moved=parts.size,
+    )
     return call(
-        functools.partial(join_kernel, segments, steps * assets), "join",
+        functools.partial(join_kernel, steps * assets), "join",
         jax.ShapeDtypeStruct((width, paths), jnp.float32),
-        [parts] + [arrived[k] for k in range(1, segments)],
-        scratch=[pltpu.VMEM((segments, 4, width, paths), jnp.float32)],
-        moved=4 * parts.size,
+        [parts] + [arrived[k] for k in range(1, segments // 2)] + [far], moved=4 * parts.size,
     )
 
 

time: 19.9 us -> 19.8 us (level)
    pallas_call x6 -> x7, Pallas kernels: 3.63 us -> 3.65 us  [call(): pl.pallas_call(kernel, out_shape=out_shape, in_specs=[HBM if i in kept el...]
where the time goes in v6:
time: 19.8 us; the launch traced here: 19.7 us
  starting transfers between devices  9.44 us (48%)
  waiting for transfers between devices  5.5 us (28%)
  Pallas kernels  3.65 us (18%)
  local copies, waits for them, and re-layouts  0.94 us (5%)
    ppermute x3, starting transfers between devices, swap(): lax.ppermute(rows, 'paths', [(s, s ^ (bit | 1)) for s in range(count)])  5.89 us
    ppermute x3, waiting for transfers between devices, shards(): lax.ppermute(parts[k].astype(jnp.float16), 'tm', [(s, s ^ k) for s in ran...  3.88 us
    pallas_call x7, Pallas kernels, call(): pl.pallas_call(kernel, out_shape=out_shape, in_specs=[HBM if i in kept el...  3.65 us
    ppermute x3, starting transfers between devices, shards(): lax.ppermute(parts[k].astype(jnp.float16), 'tm', [(s, s ^ k) for s in ran...  3.55 us
    ppermute x3, waiting for transfers between devices, swap(): lax.ppermute(rows, 'paths', [(s, s ^ (bit | 1)) for s in range(count)])  1.62 us
    unnamed x4, local copies, waits for them, and re-layouts  0.91 us
  transfers between devices with their start and end apart: 6, of which 6 were waited for; matrix products, arithmetic and copies ran while one was open for 0% of the time, Pallas kernels for 7%

profile of v6, /device:TPU:0, one launch (start us, length us, event | category | flops | bytes accessed | tf_op | source)
XLA Modules:
  0.0 19.7 jit_solution(1123648105906655859)
XLA Ops:
  0.0 0.0 copy-start
  0.0 0.5 %collective-permute-start = (bf16[32,64]{1,0:T(8,128)(2,1)}, bf16[32,64]{1,0:T(8,128)(2,1)S(1)}, u32[]{:S(2)}, u32[]{:S(2)}) collective-permute-start(bf16[32,64]{1,0:T(8,128)(2,1)} %weights_ref.1), channel_id=1, source_target_pairs={{0,1},{1,0},{2,3},{3,2},{4,5},{5,4},{6,7},{7,6},{8,9},{9,8},{10,11... | collective-permute-start | bytes 12296 | tf_op jit(solution)/shard_map/ppermute | solution.py:39
  0.5 0.0 copy-start.1
  0.5 0.9 %copy-done.1 = bf16[32,64]{1,0:T(8,128)(2,1)S(1)} copy-done((bf16[32,64]{1,0:T(8,128)(2,1)S(1)}, bf16[32,64]{1,0:T(8,128)(2,1)}, u32[]{:S(2)}) %copy-start.1) | copy-done | bytes 4120
  1.4 0.1 collective-permute-done.other_ref
  1.5 0.1 pair.1.rows_ref
  1.6 2.7 %collective-permute-start.1 = (bf16[32,128]{1,0:T(8,128)(2,1)S(1)}, bf16[32,128]{1,0:T(8,128)(2,1)S(1)}, u32[]{:S(2)}, u32[]{:S(2)}) collective-permute-start(bf16[32,128]{1,0:T(8,128)(2,1)S(1)} %pair.1.rows_ref), channel_id=1, source_target_pairs={{0,3},{1,2},{2,1},{3,0},{4,7},{5,6},{6,5},{7,4},{8,11},{9,10},{10,... | collective-permute-start | bytes 24584 | tf_op jit(solution)/shard_map/ppermute | solution.py:39
  4.3 1.4 %collective-permute-done.1.other_ref = bf16[32,128]{1,0:T(8,128)(2,1)S(1)} collective-permute-done((bf16[32,128]{1,0:T(8,128)(2,1)S(1)}, bf16[32,128]{1,0:T(8,128)(2,1)S(1)}, u32[]{:S(2)}, u32[]{:S(2)}) %collective-permute-start.1) | collective-permute-done | bytes 8224 | tf_op jit(solution)/shard_map/ppermute | solution.py:39
  5.7 2.7 %collective-permute-start.2 = (bf16[64,128]{1,0:T(8,128)(2,1)S(1)}, bf16[64,128]{1,0:T(8,128)(2,1)S(1)}, u32[]{:S(2)}, u32[]{:S(2)}) collective-permute-start(bf16[64,128]{1,0:T(8,128)(2,1)S(1)} %merge2.1.rows_ref), channel_id=1, source_target_pairs={{0,5},{1,4},{2,7},{3,6},{4,1},{5,0},{6,3},{7,2},{8,13},{9,12},{10,... | collective-permute-start | bytes 49160 | tf_op jit(solution)/shard_map/ppermute | solution.py:39
  8.4 0.0 copy-done
  8.4 1.3 %first.1.first_ref = f32[32,256,128]{2,1,0:T(8,128)S(1)} custom-call(bf16[64,128]{1,0:T(8,128)(2,1)S(1)} %merge2.1.rows_ref, bf16[32,512,256]{2,1,0:T(8,128)(2,1)S(1)} %copy-done), custom_call_target="tpu_custom_call" | custom-call | flops 536870912 | bytes 4194304 | tf_op jit(solution)/shard_map/first/pallas_call | solution.py:25
  9.7 0.1 collective-permute-done.2.rows_ref
  9.8 1.5 %second.1.own_ref = f32[4,4,16,512]{3,2,1,0:T(8,128)S(1)} custom-call(bf16[64,128]{1,0:T(8,128)(2,1)S(1)} %collective-permute-done.2.rows_ref, bf16[32,512,256]{2,1,0:T(8,128)(2,1)S(1)} %copy-done, f32[32,256,128]{2,1,0:T(8,128)S(1)} %first.1.first_ref), custom_call_target="tpu_custom_call" | custom-call | flops 536870912 | bytes 4194304 | tf_op jit(solution)/shard_map/second/pallas_call | solution.py:25
  11.5 2.8 %collective-permute-start.5 = (f16[4,16,512]{2,1,0:T(8,128)(2,1)S(1)}, f16[4,16,512]{2,1,0:T(8,128)(2,1)S(1)}, u32[]{:S(2)}, u32[]{:S(2)}) collective-permute-start(f16[4,16,512]{2,1,0:T(8,128)(2,1)S(1)} %get-tuple-element.5), channel_id=1, source_target_pairs={{0,24},{8,16},{16,8},{24,0},{1,25},{9,17},{17,9},{25,1},{2,26},{10... | collective-permute-start | bytes 196616 | tf_op jit(solution)/shard_map/ppermute | solution.py:217
  14.2 0.5 %collective-permute-start.4 = (f16[4,16,512]{2,1,0:T(8,128)(2,1)S(1)}, f16[4,16,512]{2,1,0:T(8,128)(2,1)S(1)}, u32[]{:S(2)}, u32[]{:S(2)}) collective-permute-start(f16[4,16,512]{2,1,0:T(8,128)(2,1)S(1)} %get-tuple-element.6), channel_id=1, source_target_pairs={{0,16},{8,24},{16,0},{24,8},{1,17},{9,25},{17,1},{25,9},{2,18},{10... | collective-permute-start | bytes 196616 | tf_op jit(solution)/shard_map/ppermute | solution.py:217
  14.7 0.3 %collective-permute-start.3 = (f16[4,16,512]{2,1,0:T(8,128)(2,1)S(1)}, f16[4,16,512]{2,1,0:T(8,128)(2,1)S(1)}, u32[]{:S(2)}, u32[]{:S(2)}) collective-permute-start(f16[4,16,512]{2,1,0:T(8,128)(2,1)S(1)} %get-tuple-element.7), channel_id=1, source_target_pairs={{0,8},{8,0},{16,24},{24,16},{1,9},{9,1},{17,25},{25,17},{2,10},{10... | collective-permute-start | bytes 196616 | tf_op jit(solution)/shard_map/ppermute | solution.py:217
  15.0 1.7 %collective-permute-done.5 = f16[4,16,512]{2,1,0:T(8,128)(2,1)S(1)} collective-permute-done((f16[4,16,512]{2,1,0:T(8,128)(2,1)S(1)}, f16[4,16,512]{2,1,0:T(8,128)(2,1)S(1)}, u32[]{:S(2)}, u32[]{:S(2)}) %collective-permute-start.5) | collective-permute-done | bytes 65568 | tf_op jit(solution)/shard_map/ppermute | solution.py:217
  16.7 1.7 %collective-permute-done.4 = f16[4,16,512]{2,1,0:T(8,128)(2,1)S(1)} collective-permute-done((f16[4,16,512]{2,1,0:T(8,128)(2,1)S(1)}, f16[4,16,512]{2,1,0:T(8,128)(2,1)S(1)}, u32[]{:S(2)}, u32[]{:S(2)}) %collective-permute-start.4) | collective-permute-done | bytes 65568 | tf_op jit(solution)/shard_map/ppermute | solution.py:217
  18.5 0.1 far.1.refs_1_
  18.6 0.4 %collective-permute-done.3 = f16[4,16,512]{2,1,0:T(8,128)(2,1)S(1)} collective-permute-done((f16[4,16,512]{2,1,0:T(8,128)(2,1)S(1)}, f16[4,16,512]{2,1,0:T(8,128)(2,1)S(1)}, u32[]{:S(2)}, u32[]{:S(2)}) %collective-permute-start.3) | collective-permute-done | bytes 65568 | tf_op jit(solution)/shard_map/ppermute | solution.py:217
  19.0 0.7 %join.1 = f32[16,512]{1,0:T(8,128)} custom-call(f32[4,4,16,512]{3,2,1,0:T(8,128)S(1)} %second.1.own_ref, f32[4,16,512]{2,1,0:T(8,128)S(1)} %convert_element_type.22.refs_0_, f32[4,16,512]{2,1,0:T(8,128)S(1)} %far.1.refs_1_), custom_call_target="tpu_custom_call" | custom-call | bytes 524288 | tf_op jit(solution)/shard_map/join/pallas_call | solution.py:25
  (7 shorter events, 0.1 us)
Async XLA Ops:
  0.0 8.4 %copy-start = (bf16[32,512,256]{2,1,0:T(8,128)(2,1)S(1)}, bf16[32,512,256]{2,1,0:T(8,128)(2,1)}, u32[]{:S(2)}) copy-start(bf16[32,512,256]{2,1,0:T(8,128)(2,1)} %returns_ref.5) | copy-start | bytes 25165828
  0.0 1.5 %collective-permute-start = (bf16[32,64]{1,0:T(8,128)(2,1)}, bf16[32,64]{1,0:T(8,128)(2,1)S(1)}, u32[]{:S(2)}, u32[]{:S(2)}) collective-permute-start(bf16[32,64]{1,0:T(8,128)(2,1)} %weights_ref.1), channel_id=1, source_target_pairs={{0,1},{1,0},{2,3},{3,2},{4,5},{5,4},{6,7},{7,6},{8,9},{9,8},{10,11... | collective-permute-start | bytes 12296 | tf_op jit(solution)/shard_map/ppermute | solution.py:39
  0.5 0.9 %copy-start.1 = (bf16[32,64]{1,0:T(8,128)(2,1)S(1)}, bf16[32,64]{1,0:T(8,128)(2,1)}, u32[]{:S(2)}) copy-start(bf16[32,64]{1,0:T(8,128)(2,1)} %weights_ref.1) | copy-start | bytes 12292
  1.6 4.0 %collective-permute-start.1 = (bf16[32,128]{1,0:T(8,128)(2,1)S(1)}, bf16[32,128]{1,0:T(8,128)(2,1)S(1)}, u32[]{:S(2)}, u32[]{:S(2)}) collective-permute-start(bf16[32,128]{1,0:T(8,128)(2,1)S(1)} %pair.1.rows_ref), channel_id=1, source_target_pairs={{0,3},{1,2},{2,1},{3,0},{4,7},{5,6},{6,5},{7,4},{8,11},{9,10},{10,... | collective-permute-start | bytes 24584 | tf_op jit(solution)/shard_map/ppermute | solution.py:39
  5.7 4.2 %collective-permute-start.2 = (bf16[64,128]{1,0:T(8,128)(2,1)S(1)}, bf16[64,128]{1,0:T(8,128)(2,1)S(1)}, u32[]{:S(2)}, u32[]{:S(2)}) collective-permute-start(bf16[64,128]{1,0:T(8,128)(2,1)S(1)} %merge2.1.rows_ref), channel_id=1, source_target_pairs={{0,5},{1,4},{2,7},{3,6},{4,1},{5,0},{6,3},{7,2},{8,13},{9,12},{10,... | collective-permute-start | bytes 49160 | tf_op jit(solution)/shard_map/ppermute | solution.py:39
  11.5 5.3 %collective-permute-start.5 = (f16[4,16,512]{2,1,0:T(8,128)(2,1)S(1)}, f16[4,16,512]{2,1,0:T(8,128)(2,1)S(1)}, u32[]{:S(2)}, u32[]{:S(2)}) collective-permute-start(f16[4,16,512]{2,1,0:T(8,128)(2,1)S(1)} %get-tuple-element.5), channel_id=1, source_target_pairs={{0,24},{8,16},{16,8},{24,0},{1,25},{9,17},{17,9},{25,1},{2,26},{10... | collective-permute-start | bytes 196616 | tf_op jit(solution)/shard_map/ppermute | solution.py:217
  14.2 4.3 %collective-permute-start.4 = (f16[4,16,512]{2,1,0:T(8,128)(2,1)S(1)}, f16[4,16,512]{2,1,0:T(8,128)(2,1)S(1)}, u32[]{:S(2)}, u32[]{:S(2)}) collective-permute-start(f16[4,16,512]{2,1,0:T(8,128)(2,1)S(1)} %get-tuple-element.6), channel_id=1, source_target_pairs={{0,16},{8,24},{16,0},{24,8},{1,17},{9,25},{17,1},{25,9},{2,18},{10... | collective-permute-start | bytes 196616 | tf_op jit(solution)/shard_map/ppermute | solution.py:217
  14.7 4.3 %collective-permute-start.3 = (f16[4,16,512]{2,1,0:T(8,128)(2,1)S(1)}, f16[4,16,512]{2,1,0:T(8,128)(2,1)S(1)}, u32[]{:S(2)}, u32[]{:S(2)}) collective-permute-start(f16[4,16,512]{2,1,0:T(8,128)(2,1)S(1)} %get-tuple-element.7), channel_id=1, source_target_pairs={{0,8},{8,0},{16,24},{24,16},{1,9},{9,1},{17,25},{25,17},{2,10},{10... | collective-permute-start | bytes 196616 | tf_op jit(solution)/shard_map/ppermute | solution.py:217

commit v7 on v6

--- a/solution.py
+++ b/solution.py
@@ -8,6 +8,7 @@
 from jax.experimental.pallas import tpu as pltpu
 from jax.sharding import PartitionSpec as P
 
+
 SMALLEST = 2.0**-14
 FINER = 2.0**28
 MAX_RETURN = 0.15917969
@@ -16,7 +17,7 @@
 HBM = pl.BlockSpec(memory_space=pltpu.HBM)
 
 
-def call(kernel, name, out_shape, args, scratch=(), kept=(), limit=8, flops=0, moved=0):
+def call(kernel, out_shape, args, scratch=(), kept=(), limit=8, flops=0, moved=0):
     args = [
         pltpu.with_memory_space_constraint(a, pltpu.HBM) if i in kept else a
         for i, a in enumerate(args)
@@ -30,7 +31,6 @@
         scratch_shapes=list(scratch),
         compiler_params=pltpu.CompilerParams(vmem_limit_bytes=limit * 2**20),
         cost_estimate=pl.CostEstimate(flops=flops, bytes_accessed=moved, transcendentals=0),
-        name=name,
     )(*args)
 
 
@@ -187,45 +187,44 @@
     work = 2 * steps * paths * assets * ports
 
     rows = call(
-        stage_kernel, "stage", jax.ShapeDtypeStruct(weights.shape, weights.dtype),
+        stage_kernel, jax.ShapeDtypeStruct(weights.shape, weights.dtype),
         [weights, returns], kept=(1,), flops=work, moved=returns.size * 2,
     )
     rows = call(
-        pair_kernel, "pair", jax.ShapeDtypeStruct((shard, 2 * ports), rows.dtype),
+        pair_kernel, jax.ShapeDtypeStruct((shard, 2 * ports), rows.dtype),
         [rows, swap(weights, 1)],
     )
     bit = 2
     while 2 * bit < count:
         rows = call(
-            functools.partial(merge_kernel, bit), f"merge{bit}",
+            functools.partial(merge_kernel, bit),
             jax.ShapeDtypeStruct((2 * rows.shape[0], 2 * ports), rows.dtype),
             [rows, swap(rows, bit)],
         )
         bit *= 2
     other = swap(rows, bit)
     first = call(
-        functools.partial(first_kernel, shard), "first", held, [rows, returns], scratch=[both],
+        functools.partial(first_kernel, shard), held, [rows, returns], scratch=[both],
         flops=work, moved=returns.size,
     )
     parts = call(
-        functools.partial(second_kernel, segments, shard, min(steps, 32)), "second",
+        functools.partial(second_kernel, segments, shard, min(steps, 32)),
         jax.ShapeDtypeStruct((segments, 4, width, paths), jnp.float32), [other, returns, first],
         scratch=[both, pltpu.VMEM((4, paths // 2, 2 * ports), jnp.float32)],
         flops=work, moved=returns.size,
     )
-    arrived = {
-        k: lax.ppermute(
-            parts[k].astype(jnp.float16), "tm", [(s, s ^ k) for s in range(segments)]
-        ).astype(jnp.float32)
-        for k in range(1, segments)
-    }
+    arrived = {}
+    for k in range(1, segments):
+        sent = lax.optimization_barrier(parts[k]).astype(jnp.float16)
+        pairs = [(s, s ^ k) for s in range(segments)]
+        arrived[k] = lax.ppermute(sent, "tm", pairs).astype(jnp.float32)
     far = call(
-        functools.partial(far_kernel, steps * assets), "far",
+        functools.partial(far_kernel, steps * assets),
         jax.ShapeDtypeStruct((4, width, paths), jnp.float32),
         [arrived[k] for k in range(segments // 2, segments)], moved=parts.size,
     )
     return call(
-        functools.partial(join_kernel, steps * assets), "join",
+        functools.partial(join_kernel, steps * assets),
         jax.ShapeDtypeStruct((width, paths), jnp.float32),
         [parts] + [arrived[k] for k in range(1, segments // 2)] + [far], moved=4 * parts.size,
     )
@@ -234,4 +233,6 @@
 def solution(mesh):
     in_specs = (P("tm", "paths", None), P("paths", None))
     out_specs = P("tm", "paths")
-    return jax.shard_map(shards, mesh=mesh, in_specs=in_specs, out_specs=out_specs, check_vma=False)
+    return jax.shard_map(
+        shards, mesh=mesh, in_specs=in_specs, out_specs=out_specs, check_vma=False
+    )

time: 19.8 us -> 19.9 us (level)
  transfers between devices with their start and end apart: 6 -> 6, of which waited for: 6 -> 5; matrix products, arithmetic and copies ran while one was open for 0% -> 0% of each run, Pallas kernels for 7% -> 7%
where the time goes in v7:
time: 19.9 us; the launch traced here: 19.7 us
  starting transfers between devices  9.51 us (48%)
  waiting for transfers between devices  5.5 us (28%)
  Pallas kernels  3.65 us (18%)
  local copies, waits for them, and re-layouts  0.93 us (5%)
    ppermute x3, starting transfers between devices, swap(): lax.ppermute(rows, 'paths', [(s, s ^ (bit | 1)) for s in range(count)])  5.89 us
    ppermute x3, waiting for transfers between devices, shards(): arrived[k] = lax.ppermute(sent, 'tm', pairs).astype(jnp.float32)  3.88 us
    pallas_call x7, Pallas kernels, call(): pl.pallas_call(kernel, out_shape=out_shape, in_specs=[HBM if i in kept el...  3.65 us
    ppermute x3, starting transfers between devices, shards(): arrived[k] = lax.ppermute(sent, 'tm', pairs).astype(jnp.float32)  3.62 us
    ppermute x3, waiting for transfers between devices, swap(): lax.ppermute(rows, 'paths', [(s, s ^ (bit | 1)) for s in range(count)])  1.62 us
    unnamed x4, local copies, waits for them, and re-layouts  0.91 us
  transfers between devices with their start and end apart: 6, of which 5 were waited for; matrix products, arithmetic and copies ran while one was open for 0% of the time, Pallas kernels for 7%

profile of v7, /device:TPU:0, one launch (start us, length us, event | category | flops | bytes accessed | tf_op | source)
XLA Modules:
  0.0 19.7 jit_solution(8531244432789584593)
XLA Ops:
  0.0 0.0 copy-start
  0.0 0.5 %collective-permute-start = (bf16[32,64]{1,0:T(8,128)(2,1)}, bf16[32,64]{1,0:T(8,128)(2,1)S(1)}, u32[]{:S(2)}, u32[]{:S(2)}) collective-permute-start(bf16[32,64]{1,0:T(8,128)(2,1)} %weights_ref.1), channel_id=1, source_target_pairs={{0,1},{1,0},{2,3},{3,2},{4,5},{5,4},{6,7},{7,6},{8,9},{9,8},{10,11... | collective-permute-start | bytes 12296 | tf_op jit(solution)/shard_map/ppermute | solution.py:39
  0.5 0.0 copy-start.1
  0.5 0.9 %copy-done.1 = bf16[32,64]{1,0:T(8,128)(2,1)S(1)} copy-done((bf16[32,64]{1,0:T(8,128)(2,1)S(1)}, bf16[32,64]{1,0:T(8,128)(2,1)}, u32[]{:S(2)}) %copy-start.1) | copy-done | bytes 4120
  1.4 0.1 collective-permute-done.other_ref
  1.5 0.1 shard_map.29.rows_ref
  1.6 2.7 %collective-permute-start.1 = (bf16[32,128]{1,0:T(8,128)(2,1)S(1)}, bf16[32,128]{1,0:T(8,128)(2,1)S(1)}, u32[]{:S(2)}, u32[]{:S(2)}) collective-permute-start(bf16[32,128]{1,0:T(8,128)(2,1)S(1)} %shard_map.29.rows_ref), channel_id=1, source_target_pairs={{0,3},{1,2},{2,1},{3,0},{4,7},{5,6},{6,5},{7,4},{8,11},{9,10},{10,... | collective-permute-start | bytes 24584 | tf_op jit(solution)/shard_map/ppermute | solution.py:39
  4.3 1.4 %collective-permute-done.1.other_ref = bf16[32,128]{1,0:T(8,128)(2,1)S(1)} collective-permute-done((bf16[32,128]{1,0:T(8,128)(2,1)S(1)}, bf16[32,128]{1,0:T(8,128)(2,1)S(1)}, u32[]{:S(2)}, u32[]{:S(2)}) %collective-permute-start.1) | collective-permute-done | bytes 8224 | tf_op jit(solution)/shard_map/ppermute | solution.py:39
  5.7 2.7 %collective-permute-start.2 = (bf16[64,128]{1,0:T(8,128)(2,1)S(1)}, bf16[64,128]{1,0:T(8,128)(2,1)S(1)}, u32[]{:S(2)}, u32[]{:S(2)}) collective-permute-start(bf16[64,128]{1,0:T(8,128)(2,1)S(1)} %shard_map.30.rows_ref), channel_id=1, source_target_pairs={{0,5},{1,4},{2,7},{3,6},{4,1},{5,0},{6,3},{7,2},{8,13},{9,12},{10,... | collective-permute-start | bytes 49160 | tf_op jit(solution)/shard_map/ppermute | solution.py:39
  8.4 0.0 copy-done
  8.4 1.3 %shard_map.31.first_ref = f32[32,256,128]{2,1,0:T(8,128)S(1)} custom-call(bf16[64,128]{1,0:T(8,128)(2,1)S(1)} %shard_map.30.rows_ref, bf16[32,512,256]{2,1,0:T(8,128)(2,1)S(1)} %copy-done), custom_call_target="tpu_custom_call" | custom-call | flops 536870912 | bytes 4194304 | tf_op jit(solution)/shard_map/pallas_call | solution.py:26
  9.7 0.1 collective-permute-done.2.rows_ref
  9.8 1.5 %shard_map.32.own_ref = f32[4,4,16,512]{3,2,1,0:T(8,128)S(1)} custom-call(bf16[64,128]{1,0:T(8,128)(2,1)S(1)} %collective-permute-done.2.rows_ref, bf16[32,512,256]{2,1,0:T(8,128)(2,1)S(1)} %copy-done, f32[32,256,128]{2,1,0:T(8,128)S(1)} %shard_map.31.first_ref), custom_call_target="tpu_custom_call" | custom-call | flops 536870912 | bytes 4194304 | tf_op jit(solution)/shard_map/pallas_call | solution.py:26
  11.4 1.8 %collective-permute-start.4 = (f16[4,16,512]{2,1,0:T(8,128)(2,1)S(1)}, f16[4,16,512]{2,1,0:T(8,128)(2,1)S(1)}, u32[]{:S(2)}, u32[]{:S(2)}) collective-permute-start(f16[4,16,512]{2,1,0:T(8,128)(2,1)S(1)} %convert_element_type.20), channel_id=1, source_target_pairs={{0,16},{8,24},{16,0},{24,8},{1,17},{9,25},{17,1},{25,9},{2,18},{10... | collective-permute-start | bytes 196616 | tf_op jit(solution)/shard_map/ppermute | solution.py:220
  13.3 1.4 %collective-permute-start.5 = (f16[4,16,512]{2,1,0:T(8,128)(2,1)S(1)}, f16[4,16,512]{2,1,0:T(8,128)(2,1)S(1)}, u32[]{:S(2)}, u32[]{:S(2)}) collective-permute-start(f16[4,16,512]{2,1,0:T(8,128)(2,1)S(1)} %convert_element_type.22), channel_id=1, source_target_pairs={{0,24},{8,16},{16,8},{24,0},{1,25},{9,17},{17,9},{25,1},{2,26},{10... | collective-permute-start | bytes 196616 | tf_op jit(solution)/shard_map/ppermute | solution.py:220
  14.7 0.3 %collective-permute-start.3 = (f16[4,16,512]{2,1,0:T(8,128)(2,1)S(1)}, f16[4,16,512]{2,1,0:T(8,128)(2,1)S(1)}, u32[]{:S(2)}, u32[]{:S(2)}) collective-permute-start(f16[4,16,512]{2,1,0:T(8,128)(2,1)S(1)} %convert_element_type.18), channel_id=1, source_target_pairs={{0,8},{8,0},{16,24},{24,16},{1,9},{9,1},{17,25},{25,17},{2,10},{10... | collective-permute-start | bytes 196616 | tf_op jit(solution)/shard_map/ppermute | solution.py:220
  15.1 1.3 %collective-permute-done.4 = f16[4,16,512]{2,1,0:T(8,128)(2,1)S(1)} collective-permute-done((f16[4,16,512]{2,1,0:T(8,128)(2,1)S(1)}, f16[4,16,512]{2,1,0:T(8,128)(2,1)S(1)}, u32[]{:S(2)}, u32[]{:S(2)}) %collective-permute-start.4) | collective-permute-done | bytes 65568 | tf_op jit(solution)/shard_map/ppermute | solution.py:220
  16.4 2.6 %collective-permute-done.5 = f16[4,16,512]{2,1,0:T(8,128)(2,1)S(1)} collective-permute-done((f16[4,16,512]{2,1,0:T(8,128)(2,1)S(1)}, f16[4,16,512]{2,1,0:T(8,128)(2,1)S(1)}, u32[]{:S(2)}, u32[]{:S(2)}) %collective-permute-start.5) | collective-permute-done | bytes 65568 | tf_op jit(solution)/shard_map/ppermute | solution.py:220
  19.0 0.1 shard_map.33.refs_1_
  19.0 0.0 collective-permute-done.3
  19.1 0.7 %shard_map.34 = f32[16,512]{1,0:T(8,128)} custom-call(f32[4,4,16,512]{3,2,1,0:T(8,128)S(1)} %shard_map.32.own_ref, f32[4,16,512]{2,1,0:T(8,128)S(1)} %convert_element_type.19.refs_0_, f32[4,16,512]{2,1,0:T(8,128)S(1)} %shard_map.33.refs_1_), custom_call_target="tpu_custom_call" | custom-call | bytes 524288 | tf_op jit(solution)/shard_map/pallas_call | solution.py:26
  (9 shorter events, 0.1 us)
Async XLA Ops:
  0.0 8.4 %copy-start = (bf16[32,512,256]{2,1,0:T(8,128)(2,1)S(1)}, bf16[32,512,256]{2,1,0:T(8,128)(2,1)}, u32[]{:S(2)}) copy-start(bf16[32,512,256]{2,1,0:T(8,128)(2,1)} %returns_ref.5) | copy-start | bytes 25165828
  0.0 1.5 %collective-permute-start = (bf16[32,64]{1,0:T(8,128)(2,1)}, bf16[32,64]{1,0:T(8,128)(2,1)S(1)}, u32[]{:S(2)}, u32[]{:S(2)}) collective-permute-start(bf16[32,64]{1,0:T(8,128)(2,1)} %weights_ref.1), channel_id=1, source_target_pairs={{0,1},{1,0},{2,3},{3,2},{4,5},{5,4},{6,7},{7,6},{8,9},{9,8},{10,11... | collective-permute-start | bytes 12296 | tf_op jit(solution)/shard_map/ppermute | solution.py:39
  0.5 0.9 %copy-start.1 = (bf16[32,64]{1,0:T(8,128)(2,1)S(1)}, bf16[32,64]{1,0:T(8,128)(2,1)}, u32[]{:S(2)}) copy-start(bf16[32,64]{1,0:T(8,128)(2,1)} %weights_ref.1) | copy-start | bytes 12292
  1.6 4.0 %collective-permute-start.1 = (bf16[32,128]{1,0:T(8,128)(2,1)S(1)}, bf16[32,128]{1,0:T(8,128)(2,1)S(1)}, u32[]{:S(2)}, u32[]{:S(2)}) collective-permute-start(bf16[32,128]{1,0:T(8,128)(2,1)S(1)} %shard_map.29.rows_ref), channel_id=1, source_target_pairs={{0,3},{1,2},{2,1},{3,0},{4,7},{5,6},{6,5},{7,4},{8,11},{9,10},{10,... | collective-permute-start | bytes 24584 | tf_op jit(solution)/shard_map/ppermute | solution.py:39
  5.7 4.2 %collective-permute-start.2 = (bf16[64,128]{1,0:T(8,128)(2,1)S(1)}, bf16[64,128]{1,0:T(8,128)(2,1)S(1)}, u32[]{:S(2)}, u32[]{:S(2)}) collective-permute-start(bf16[64,128]{1,0:T(8,128)(2,1)S(1)} %shard_map.30.rows_ref), channel_id=1, source_target_pairs={{0,5},{1,4},{2,7},{3,6},{4,1},{5,0},{6,3},{7,2},{8,13},{9,12},{10,... | collective-permute-start | bytes 49160 | tf_op jit(solution)/shard_map/ppermute | solution.py:39
  11.4 4.9 %collective-permute-start.4 = (f16[4,16,512]{2,1,0:T(8,128)(2,1)S(1)}, f16[4,16,512]{2,1,0:T(8,128)(2,1)S(1)}, u32[]{:S(2)}, u32[]{:S(2)}) collective-permute-start(f16[4,16,512]{2,1,0:T(8,128)(2,1)S(1)} %convert_element_type.20), channel_id=1, source_target_pairs={{0,16},{8,24},{16,0},{24,8},{1,17},{9,25},{17,1},{25,9},{2,18},{10... | collective-permute-start | bytes 196616 | tf_op jit(solution)/shard_map/ppermute | solution.py:220
  13.3 5.7 %collective-permute-start.5 = (f16[4,16,512]{2,1,0:T(8,128)(2,1)S(1)}, f16[4,16,512]{2,1,0:T(8,128)(2,1)S(1)}, u32[]{:S(2)}, u32[]{:S(2)}) collective-permute-start(f16[4,16,512]{2,1,0:T(8,128)(2,1)S(1)} %convert_element_type.22), channel_id=1, source_target_pairs={{0,24},{8,16},{16,8},{24,0},{1,25},{9,17},{17,9},{25,1},{2,26},{10... | collective-permute-start | bytes 196616 | tf_op jit(solution)/shard_map/ppermute | solution.py:220
  14.7 4.3 %collective-permute-start.3 = (f16[4,16,512]{2,1,0:T(8,128)(2,1)S(1)}, f16[4,16,512]{2,1,0:T(8,128)(2,1)S(1)}, u32[]{:S(2)}, u32[]{:S(2)}) collective-permute-start(f16[4,16,512]{2,1,0:T(8,128)(2,1)S(1)} %convert_element_type.18), channel_id=1, source_target_pairs={{0,8},{8,0},{16,24},{24,16},{1,9},{9,1},{17,25},{25,17},{2,10},{10... | collective-permute-start | bytes 196616 | tf_op jit(solution)/shard_map/ppermute | solution.py:220
